TPU v7x, 32 devices: a 4x4x1 block of a 4x4x8 slice. The times are simulated.
32 devices in a mesh: data: 1 (over z), feat: 4 (over y), graph: 8 (over x, core).
Axes of the slice: x: 4, y: 4, z: 1, core: 2. Of those that a mesh axis runs over, the one named last changes fastest.
The devices are a block of a 4x4x8 slice.
Arguments:
- X: bfloat16 [16384, 300], P(('data', 'graph'), 'feat')
- dst_local: int32 [327680], P(('data', 'graph'))
- src_slot: int32 [327680], P(('data', 'graph'))
- valid: int32 [327680], P(('data', 'graph'))
- w: float32 [327680], P(('data', 'graph'))
- send_idx: int32 [64, 256], P(('data', 'graph'))
- send_valid: int32 [64, 256], P(('data', 'graph'))
- hub_ids: int32 [128], P('data')
- W1: bfloat16 [300, 512], P('feat')
- W2: bfloat16 [512, 512], P('feat')
- b1: float32 [512], P('feat')
- b2: float32 [512], P('feat')
Outputs:
- output: float32 [16384, 512], P(('data', 'graph'), 'feat')
All inputs are finite; a program needn't handle non-finite values.
Results may differ from a plain program's by a relative error of at most 0.001.
Values are sent between devices in bfloat16 or wider.
A program may use at most 768 MiB of HBM per device.

v0:
```python
import functools

import jax
import jax.numpy as jnp
from jax import lax
from jax.experimental import pallas as pl
from jax.experimental.pallas import tpu as pltpu
from jax.sharding import PartitionSpec as P

DB, SB, KW = 128, 256, 256
MESH = pl.DeviceIdType.MESH
F32, BF16 = jnp.float32, jnp.bfloat16


def bf16_parts(x):
    hi = x.astype(BF16)
    rest = x - hi.astype(F32)
    mid = rest.astype(BF16)
    low = (rest - mid.astype(F32)).astype(BF16)
    return hi, mid, low


def build_kernel(nsb, starts_ref, edges_ref, rowid_ref, colid_ref, a_ref):
    db = pl.program_id(0)
    dbase = (db * DB).astype(F32)
    row_id = rowid_ref[0]
    iota_s = lax.broadcasted_iota(jnp.int32, (SB, KW), 0).astype(BF16)
    zero = jnp.zeros((), BF16)

    def window(sb, start):
        base = pl.multiple_of((start // 128) * 128, 128)
        shift = start - base
        raw = edges_ref[:, pl.ds(base, KW + 128)]
        rows = pltpu.roll(raw, KW + 128 - shift, 1)[:, :KW]
        dst = (rows[0:1] - dbase).astype(BF16)
        src = (rows[1:2] - F32(SB * sb)).astype(BF16)
        hit = row_id == dst
        d3 = jnp.concatenate([jnp.where(hit, part, zero) for part in bf16_parts(rows[2:3])], axis=0)
        col_id = colid_ref[...] if sb == nsb - 1 else iota_s
        sel = jnp.where(col_id == src, jnp.ones((), BF16), zero)
        out = lax.dot_general(d3, sel, (((1,), (1,)), ((), ())), preferred_element_type=F32)
        return out[:DB] + (out[DB:2 * DB] + out[2 * DB:])

    for sb in range(nsb):
        a_ref[:, sb * SB:(sb + 1) * SB] = window(sb, starts_ref[db * nsb + sb])
    for sb in range(nsb):
        start = starts_ref[db * nsb + sb]
        end = starts_ref[db * nsb + sb + 1]

        def more(i, carry):
            a_ref[:, sb * SB:(sb + 1) * SB] += window(sb, start + i * KW)
            return carry

        lax.fori_loop(1, (end - start + KW - 1) // KW, more, 0)


def build_adjacency(starts, edges, rowid, colid, ndb, nsb):
    return pl.pallas_call(
        functools.partial(build_kernel, nsb),
        out_shape=jax.ShapeDtypeStruct((ndb * DB, nsb * SB), F32),
        grid_spec=pltpu.PrefetchScalarGridSpec(
            num_scalar_prefetch=1,
            grid=(ndb,),
            in_specs=[
                pl.BlockSpec(edges.shape, lambda i, s: (0, 0)),
                pl.BlockSpec((1, DB, KW), lambda i, s: (i // (ndb - 1), 0, 0)),
                pl.BlockSpec(colid.shape, lambda i, s: (0, 0)),
            ],
            out_specs=pl.BlockSpec((DB, nsb * SB), lambda i, s: (i, 0)),
        ),
        name="build",
    )(starts, edges, rowid, colid)


def layers_kernel(dims, x_ref, w1_ref, w2_ref, idx_ref, myhub_ref, b1_ref, b2_ref, inv_ref, a_hbm, o_ref,
                  a_v, xin, w1in, w2in, tab1, tab2, zout, hsend, hin, halo, hubsend, hubrecv,
                  a_sem, xs, xr, w1s, w1r, w2s, w2r, z1s, z1r, z2s, z2r, hs, hr, ps, pr, us, ur, ns, nr):
    nfeat, ngraph, vert, nsend, per = dims
    part, rows_send = vert // nfeat, nsend + per
    nchunk = part // DB
    f, g = lax.axis_index("feat"), lax.axis_index("graph")
    halo_base, hub_base = vert, vert + ngraph * nsend
    nblock = vert // DB

    def fpeer(r):
        return lax.rem(f + r, nfeat)

    def gpeer(r):
        return lax.rem(g + r, ngraph)

    def frdma(src, dst, send, recv, r):
        return pltpu.make_async_remote_copy(src, dst, send, recv, device_id={"feat": fpeer(r)}, device_id_type=MESH)

    def grdma(src, dst, send, recv, r):
        return pltpu.make_async_remote_copy(src, dst, send, recv, device_id={"graph": gpeer(r)}, device_id_type=MESH)

    a_copies = [pltpu.make_async_copy(a_hbm.at[pl.ds(i * DB, DB)], a_v.at[pl.ds(i * DB, DB)], a_sem.at[i]) for i in range(a_hbm.shape[0] // DB)]
    for copy in a_copies:
        copy.start()

    barrier = pltpu.get_barrier_semaphore()
    for r in range(1, nfeat):
        pl.semaphore_signal(barrier, inc=1, device_id={"feat": fpeer(r)}, device_id_type=MESH)
    for r in range(1, ngraph):
        pl.semaphore_signal(barrier, inc=1, device_id={"graph": gpeer(r)}, device_id_type=MESH)
    pl.semaphore_wait(barrier, nfeat + ngraph - 2)

    def quarter(q):
        return pl.ds(pl.multiple_of(q * part, part), part)

    x_copies = [frdma(x_ref.at[quarter(fpeer(r))], xin.at[f], xs.at[r - 1], xr.at[r - 1], r) for r in range(1, nfeat)]
    w1_copies = [frdma(w1_ref, w1in.at[f], w1s.at[r - 1], w1r.at[r - 1], r) for r in range(1, nfeat)]
    w2_copies = [frdma(w2_ref, w2in.at[f], w2s.at[r - 1], w2r.at[r - 1], r) for r in range(1, nfeat)]
    for copy in w1_copies + x_copies + w2_copies:
        copy.start()
    xin[f] = x_ref[quarter(f)]
    w1in[f] = w1_ref[...]
    w2in[f] = w2_ref[...]
    pad_rows = a_v.shape[1] - hub_base - ngraph * per
    for tab in (tab1, tab2):
        tab[pl.ds(pl.multiple_of(halo_base + g * nsend, nsend), nsend)] = jnp.zeros((nsend, tab.shape[1]), BF16)
        tab[hub_base + ngraph * per:] = jnp.zeros((pad_rows, tab.shape[1]), BF16)

    for copy in w1_copies + x_copies:
        copy.wait_recv()
    cols = tab1.shape[1]
    z = None
    for s in range(nfeat):
        term = jnp.dot(xin[s], w1in[s], preferred_element_type=F32)
        z = term if z is None else z + term
    z = z.astype(BF16)
    for q in range(nfeat):
        zout[q] = z[:, q * cols:(q + 1) * cols]
    z1_copies = [frdma(zout.at[fpeer(r)], tab1.at[quarter(f)], z1s.at[r - 1], z1r.at[r - 1], r) for r in range(1, nfeat)]
    for copy in z1_copies:
        copy.start()
    tab1[quarter(f)] = zout[f]
    for copy in z1_copies:
        copy.wait_recv()

    lane = lax.broadcasted_iota(jnp.int32, (1, DB), 1)

    def select_rows(tab, idx):
        pieces = [jnp.where(idx == lane + DB * j, F32(1), F32(0)).astype(BF16) for j in range(vert // DB)]
        return jnp.dot(jnp.concatenate(pieces, axis=1), tab[:vert], preferred_element_type=F32).astype(BF16)

    def halo_copies(tab, layer, r):
        p = gpeer(r)
        return (
            grdma(halo.at[layer, p, pl.ds(0, nsend)], tab.at[pl.ds(pl.multiple_of(halo_base + g * nsend, nsend), nsend)],
                  hs.at[layer, r - 1], hr.at[layer, r - 1], r),
            grdma(halo.at[layer, p, pl.ds(nsend, per)], tab.at[pl.ds(pl.multiple_of(hub_base + g * per, per), per)],
                  ps.at[layer, r - 1], pr.at[layer, r - 1], r),
        )

    def exchange_halo(tab, layer):
        def one(r, carry):
            p = gpeer(r)
            halo[layer, p] = select_rows(tab, idx_ref[p])
            for copy in halo_copies(tab, layer, r):
                copy.start()
            return carry

        lax.fori_loop(1, ngraph, one, 0)
        tab[pl.ds(pl.multiple_of(hub_base + g * per, per), per)] = select_rows(tab, idx_ref[g, nsend:])

        def arrive(r, carry):
            for copy in halo_copies(tab, layer, r):
                copy.wait_recv()
            return carry

        lax.fori_loop(1, ngraph, arrive, 0)

    inv = inv_ref[...]

    def block(tab, rb):
        a = a_v[pl.ds(pl.multiple_of(rb * DB, DB), DB), :]
        out = jnp.dot(jnp.concatenate(bf16_parts(a), axis=0), tab[...], preferred_element_type=F32)
        return (out[:DB] + (out[DB:2 * DB] + out[2 * DB:])) * inv

    def hub_copy(layer, r):
        p = gpeer(r)
        return grdma(hubsend.at[layer, pl.ds(pl.multiple_of(p * per, per), per)], hubrecv.at[layer, g], us.at[layer, r - 1], ur.at[layer, r - 1], r)

    def exchange_hubs(tab, layer):
        hubsend[layer] = block(tab, nblock)
        for r in range(1, ngraph):
            hub_copy(layer, r).start()
        hubrecv[layer, g] = hubsend[layer, pl.ds(pl.multiple_of(g * per, per), per)]

    def hub_totals(layer):
        for r in range(1, ngraph):
            hub_copy(layer, r).wait_recv()
        total = hubrecv[layer, 0]
        for p in range(1, ngraph):
            total = total + hubrecv[layer, p]
        fill = jnp.zeros((DB - 3 * per, total.shape[1]), BF16)
        return jnp.concatenate([*bf16_parts(total), fill], axis=0)

    def with_hubs(layer, totals, y, rb):
        rows = lax.broadcasted_iota(jnp.int32, (DB, DB), 0) + rb * DB
        sel = jnp.where(rows == myhub_ref[...], F32(1), F32(0)).astype(BF16)
        return y + jnp.dot(sel, totals, preferred_element_type=F32)

    exchange_halo(tab1, 0)
    for copy in a_copies:
        copy.wait()
    exchange_hubs(tab1, 0)
    totals1 = hub_totals(0)
    for copy in w2_copies:
        copy.wait_recv()

    def chunk(i):
        return pl.ds(pl.multiple_of(i * DB, DB), DB)

    def h_copy(i, r):
        return frdma(hsend.at[fpeer(r), chunk(i)], hin.at[f, chunk(i)], ns.at[i, r - 1], nr.at[i, r - 1], r)

    def z2_copy(i, r):
        return frdma(zout.at[fpeer(r), chunk(i)], tab2.at[pl.ds(pl.multiple_of(f * part + i * DB, DB), DB)], z2s.at[i, r - 1], z2r.at[i, r - 1], r)

    for copy in z1_copies:
        copy.wait_send()

    def z2_chunk(i):
        for r in range(1, nfeat):
            h_copy(i, r).wait_recv()
        acc = None
        for s in range(nfeat):
            term = jnp.dot(hin[s, chunk(i)], w2in[s], preferred_element_type=F32)
            acc = term if acc is None else acc + term
        acc = acc.astype(BF16)
        for q in range(nfeat):
            zout[q, chunk(i)] = acc[:, q * cols:(q + 1) * cols]
        for r in range(1, nfeat):
            z2_copy(i, r).start()
        tab2[pl.ds(pl.multiple_of(f * part + i * DB, DB), DB)] = zout[f, chunk(i)]

    bias1 = b1_ref[...]

    def rows1(t, carry):
        i, rr = t // nfeat, lax.rem(t, nfeat)
        q = fpeer(rr + 1)
        rb = q * nchunk + i
        h = jnp.maximum(with_hubs(0, totals1, block(tab1, rb), rb) + bias1, 0.0).astype(BF16)

        @pl.when(rr < nfeat - 1)
        def _():
            hsend[q, chunk(i)] = h
            h_copy(i, rr + 1).start()

        @pl.when(rr == nfeat - 1)
        def _():
            hin[f, chunk(i)] = h

        @pl.when((rr == nfeat - 2) & (i > 0))
        def _():
            z2_chunk(i - 1)

        return carry

    lax.fori_loop(0, nblock, rows1, 0)
    z2_chunk(nchunk - 1)
    for i in range(nchunk):
        for r in range(1, nfeat):
            z2_copy(i, r).wait_recv()

    exchange_halo(tab2, 1)
    exchange_hubs(tab2, 1)
    totals2 = hub_totals(1)
    bias2 = b2_ref[...]

    def rows2(rb, carry):
        o_ref[chunk(rb), :] = with_hubs(1, totals2, block(tab2, rb), rb) + bias2
        return carry

    lax.fori_loop(0, nblock, rows2, 0)

    for copy in x_copies + w1_copies + w2_copies:
        copy.wait_send()
    for i in range(nchunk):
        for r in range(1, nfeat):
            h_copy(i, r).wait_send()
            z2_copy(i, r).wait_send()
    for layer, tab in enumerate((tab1, tab2)):
        for r in range(1, ngraph):
            for copy in halo_copies(tab, layer, r):
                copy.wait_send()
            hub_copy(layer, r).wait_send()


def run_layers(nfeat, ngraph, nsend, per, x, w1, w2, idx, myhub, b1, b2, inv, adj):
    vert = x.shape[0]
    part, cols = vert // nfeat, b1.shape[1]
    nchunk, nblk = part // DB, adj.shape[0] // DB
    vm = lambda shape, dt: pltpu.VMEM(shape, dt)
    dma = lambda *shape: pltpu.SemaphoreType.DMA(shape)
    vspec = pl.BlockSpec(memory_space=pltpu.VMEM)
    fr, gr = nfeat - 1, ngraph - 1
    return pl.pallas_call(
        functools.partial(layers_kernel, (nfeat, ngraph, vert, nsend, per)),
        out_shape=jax.ShapeDtypeStruct((vert, cols), F32),
        in_specs=[vspec] * 8 + [pl.BlockSpec(memory_space=pl.ANY)],
        out_specs=vspec,
        scratch_shapes=[
            vm(adj.shape, F32), vm((nfeat, part, x.shape[1]), BF16), vm((nfeat, *w1.shape), BF16), vm((nfeat, *w2.shape), BF16),
            vm((adj.shape[1], cols), BF16), vm((adj.shape[1], cols), BF16), vm((nfeat, part, cols), BF16), vm((nfeat, part, cols), BF16),
            vm((nfeat, part, cols), BF16), vm((2, ngraph, nsend + per, cols), BF16), vm((2, ngraph * per, cols), F32), vm((2, ngraph, per, cols), F32),
            dma(nblk), dma(fr), dma(fr), dma(fr), dma(fr), dma(fr), dma(fr), dma(fr), dma(fr), dma(nchunk, fr), dma(nchunk, fr),
            dma(2, gr), dma(2, gr), dma(2, gr), dma(2, gr), dma(2, gr), dma(2, gr), dma(nchunk, fr), dma(nchunk, fr),
        ],
        compiler_params=pltpu.CompilerParams(collective_id=0, has_side_effects=True, vmem_limit_bytes=62 * 2**20),
        name="layers",
    )(x, w1, w2, idx, myhub, b1, b2, inv, adj)


def solution(mesh):
    rows_axes = ("data", "graph")
    nfeat = mesh.shape["feat"]
    ngraph = mesh.shape["graph"]

    def device_program(x_loc, dst_loc, src_loc, valid_loc, w_loc, send_loc, keep_loc, hub_ids, w_first, w_second, b_first, b_second):
        vert = x_loc.shape[0]
        nhub = hub_ids.shape[0]
        per = nhub // ngraph
        nsend = send_loc.shape[1]
        cols = b_first.shape[0]
        me = lax.axis_index("graph")
        ndb = (vert + nhub) // DB
        table_rows = vert + ngraph * nsend + nhub
        nsb = -(-table_rows // SB)

        owner = hub_ids // vert
        ks = jnp.arange(nhub)
        before = (owner[None, :] == owner[:, None]) & (ks[None, :] < ks[:, None])
        pos = owner * per + jnp.sum(before.astype(jnp.int32), axis=1)
        at_pos = pos[None, :] == ks[:, None]
        hub_by_pos = jnp.sum(jnp.where(at_pos, hub_ids[None, :], 0), axis=1)
        k_by_pos = jnp.sum(jnp.where(at_pos, ks[None, :], 0), axis=1)
        my_hubs = lax.dynamic_slice(hub_by_pos, (me * per,), (per,)) - me * vert

        key = ((dst_loc // DB) << 20) | ((src_loc // SB) << 15) | ((dst_loc % DB) << 8) | (src_loc % SB)
        key = jnp.where(valid_loc > 0, key, 1 << 26)
        coef = w_loc * valid_loc.astype(F32)
        large = jnp.max(coef) > 1e30
        coef = coef * jnp.where(large, F32(2.0**-40), F32(1))
        inv = jnp.where(large, F32(2.0**40), F32(1))
        nb = jnp.arange(ndb * nsb + 1)
        bound = ((nb // nsb) << 20) | ((nb % nsb) << 15)
        starts = jnp.sum((key[None, :] < bound[:, None]).astype(jnp.int32), axis=1)
        skey, sw = lax.sort((key, coef), num_keys=1, is_stable=False)
        sdst = (skey >> 20) * DB + ((skey >> 8) & (DB - 1))
        ssrc = ((skey >> 15) & 31) * SB + (skey & (SB - 1))
        edges = jnp.stack([sdst.astype(F32), ssrc.astype(F32), sw])
        edges = jnp.pad(edges, ((0, 5), (0, 2 * KW)), constant_values=-1.0)
        rowid = jnp.stack([jnp.arange(DB), k_by_pos]).astype(BF16)
        rowid = jnp.broadcast_to(rowid[:, :, None], (2, DB, KW))
        colid = jnp.pad(k_by_pos, (0, SB - nhub), constant_values=300).astype(BF16)
        colid = jnp.broadcast_to(colid[:, None], (SB, KW))
        adj = build_adjacency(starts, edges, rowid, colid, ndb, nsb)

        idx = jnp.where(keep_loc > 0, send_loc, -1)
        idx = jnp.concatenate([idx, jnp.broadcast_to(my_hubs[None, :], (ngraph, per))], axis=1)
        idx = jnp.broadcast_to(idx[:, :, None], (*idx.shape, DB))
        myhub = jnp.pad(jnp.concatenate([my_hubs] * 3), (0, DB - 3 * per), constant_values=-1)[None, :]
        inv = jnp.full((1, cols), inv)
        return run_layers(nfeat, ngraph, nsend, per, x_loc, w_first, w_second, idx, myhub, b_first[None, :], b_second[None, :], inv, adj)

    edge_spec = P(rows_axes)
    send_spec = P(rows_axes, None)
    in_specs = (P(rows_axes, "feat"), edge_spec, edge_spec, edge_spec, edge_spec, send_spec, send_spec, P("data"), P("feat", None), P("feat", None), P("feat"), P("feat"))
    return jax.shard_map(device_program, mesh=mesh, in_specs=in_specs, out_specs=P(rows_axes, "feat"), check_vma=False)
```

profile of v0, /device:TPU:97, one launch (start us, length us, event | category | flops | bytes accessed | tf_op | source)
XLA Modules:
  0.0 175.7 jit_solution(7059319606360859405)
XLA Ops:
  0.0 1.6 fusion.15
  2.3 1.0 broadcast_multiply_fusion
  3.3 1.4 fusion.4
  4.7 0.0 copy-start.3
  4.7 18.4 %sort.15 = (s32[40960]{0:T(1024)S(1)}, f32[40960]{0:T(1024)S(1)}) sort(s32[40960]{0:T(1024)S(1)} %fusion.4, f32[40960]{0:T(1024)S(1)} %broadcast_multiply_fusion), dimensions={0}, to_apply=%region_4.5 | sort | flops 655360 | bytes 655360 | tf_op jit(solution)/shard_map/sort | solution.py:351
  23.2 0.1 add_convert_fusion.1
  23.2 1.7 select_maximum_fusion.edges_ref
  25.0 0.0 copy-done.3
  25.0 0.2 convert_reduce_fusion.1
  25.2 0.1 select_reduce_fusion
  25.3 0.8 broadcast_in_dim.80.rowid_ref
  26.1 0.8 broadcast_in_dim.81.colid_ref
  26.9 6.5 %convert_reduce_fusion.starts_ref = s32[290]{0:T(512)} fusion(s32[40960]{0:T(1024)S(1)} %fusion.4, s32[290]{0:T(512)S(1)} %fusion.22), kind=kLoop, calls=%fused_computation | loop fusion | flops 35634912 | bytes 166160 | tf_op jit(solution)/shard_map/reduce_sum | solution.py:350
  33.3 0.0 copy-start.1
  33.3 0.0 copy-start.2
  33.3 29.6 %build.1.a_hbm = f32[2176,4352]{1,0:T(8,128)} custom-call(s32[290]{0:T(512)} %convert_reduce_fusion.starts_ref, f32[8,41472]{1,0:T(8,128)} %select_maximum_fusion.edges_ref, bf16[2,128,256]{2,1,0:T(8,128)(2,1)} %broadcast_in_dim.80.rowid_ref, bf16[256,256]{1,0:T(8,128)(2,1)} %broadcast_in_dim.81.colid_ref), custom_call_target="tpu_custom_call" | custom-call | tf_op jit(solution)/shard_map/build/pallas_call | solution.py:58
  62.9 0.0 copy-start
  62.9 0.1 dynamic-slice_subtract_fusion
  63.0 0.0 copy-done.1
  63.0 0.0 copy-done.2
  63.1 1.3 broadcast_in_dim.74.idx_ref
  64.4 0.1 pad_add_fusion.1
  64.5 0.5 pad_bitcast_fusion.myhub_ref
  65.0 0.5 broadcast_in_dim.78.inv_ref
  65.5 0.0 copy-done
  65.5 1.0 copy.14.x_ref
  66.5 106.9 %layers.1 = f32[2048,128]{1,0:T(8,128)} custom-call(bf16[2048,75]{1,0:T(8,128)(2,1)} %copy.14.x_ref, bf16[75,512]{1,0:T(8,128)(2,1)} %w1_ref.1, bf16[128,512]{1,0:T(8,128)(2,1)} %w2_ref.1, s32[8,272,128]{2,1,0:T(8,128)} %broadcast_in_dim.74.idx_ref, s32[1,128]{1,0:T(1,128)} %pad_bitcast_fusion.myhub_ref, f32[1,128]{1,0:T(1,128)} %bitcast.12, ...), custom_call_target="tpu_custom_call" | custom-call | tf_op jit(solution)/shard_map/layers/pallas_call | solution.py:300
  173.4 2.3 %copy.16 = f32[2048,128]{1,0:T(8,128)} copy(f32[2048,128]{1,0:T(8,128)} %layers.1) | data formatting | bytes 2097152
  (10 shorter events, 0.1 us)
Async XLA Ops:
  4.7 20.2 %copy-start.3 = (s32[128]{0:T(128)S(1)}, s32[128]{0:T(128)}, u32[]{:S(2)}) copy-start(s32[128]{0:T(128)} %param.19) | copy-start | bytes 1540
  33.3 29.7 %copy-start.1 = (s32[8,256]{1,0:T(8,128)S(1)}, s32[8,256]{1,0:T(8,128)}, u32[]{:S(2)}) copy-start(s32[8,256]{1,0:T(8,128)} %param.17) | copy-start | bytes 24580
  33.3 29.7 %copy-start.2 = (s32[8,256]{1,0:T(8,128)S(1)}, s32[8,256]{1,0:T(8,128)}, u32[]{:S(2)}) copy-start(s32[8,256]{1,0:T(8,128)} %param.18) | copy-start | bytes 24580
  62.9 2.6 %copy-start = (bf16[2048,75]{0,1:T(8,128)(2,1)S(1)}, bf16[2048,75]{0,1:T(8,128)(2,1)}, u32[]{:S(2)}) copy-start(bf16[2048,75]{0,1:T(8,128)(2,1)} %param.12) | copy-start | bytes 921604
where the time goes:
time: 176 us
  Pallas kernels  137 us (78%)
  other arithmetic  31.2 us (18%)
  local copies, waits for them, and re-layouts  7.2 us (4%)
    pallas_call x1, Pallas kernels, run_layers(): pl.pallas_call(functools.partial(layers_kernel, (nfeat, ngraph, vert, nse...  107 us
    pallas_call x1, Pallas kernels, build_adjacency(): pl.pallas_call(functools.partial(build_kernel, nsb), out_shape=jax.ShapeD...  29.6 us
    sort x1, other arithmetic, device_program(): skey, sw = lax.sort((key, coef), num_keys=1, is_stable=False)  18.4 us
    reduce_sum x1, other arithmetic, device_program(): starts = jnp.sum((key[None, :] < bound[:, None]).astype(jnp.int32), axis=1)  6.46 us

commit v1 on v0

--- a/solution.py
+++ b/solution.py
@@ -8,6 +8,7 @@
 from jax.sharding import PartitionSpec as P
 
 DB, SB, KW = 128, 256, 256
+LAG = 4
 MESH = pl.DeviceIdType.MESH
 F32, BF16 = jnp.float32, jnp.bfloat16
 
@@ -73,7 +74,7 @@
 
 
 def layers_kernel(dims, x_ref, w1_ref, w2_ref, idx_ref, myhub_ref, b1_ref, b2_ref, inv_ref, a_hbm, o_ref,
-                  a_v, xin, w1in, w2in, tab1, tab2, zout, hsend, hin, halo, hubsend, hubrecv,
+                  a_v, acc, tot, xin, w1in, w2in, tab1, tab2, zout, hsend, hin, halo, hubsend, hubrecv,
                   a_sem, xs, xr, w1s, w1r, w2s, w2r, z1s, z1r, z2s, z2r, hs, hr, ps, pr, us, ur, ns, nr):
     nfeat, ngraph, vert, nsend, per = dims
     part, rows_send = vert // nfeat, nsend + per
@@ -94,9 +95,8 @@
     def grdma(src, dst, send, recv, r):
         return pltpu.make_async_remote_copy(src, dst, send, recv, device_id={"graph": gpeer(r)}, device_id_type=MESH)
 
-    a_copies = [pltpu.make_async_copy(a_hbm.at[pl.ds(i * DB, DB)], a_v.at[pl.ds(i * DB, DB)], a_sem.at[i]) for i in range(a_hbm.shape[0] // DB)]
-    for copy in a_copies:
-        copy.start()
+    for i in range(a_hbm.shape[0] // DB):
+        pltpu.make_async_copy(a_hbm.at[pl.ds(i * DB, DB)], a_v.at[pl.ds(i * DB, DB)], a_sem.at[i]).start()
 
     barrier = pltpu.get_barrier_semaphore()
     for r in range(1, nfeat):
@@ -153,7 +153,7 @@
                   ps.at[layer, r - 1], pr.at[layer, r - 1], r),
         )
 
-    def exchange_halo(tab, layer):
+    def start_halo(tab, layer):
         def one(r, carry):
             p = gpeer(r)
             halo[layer, p] = select_rows(tab, idx_ref[p])
@@ -164,6 +164,7 @@
         lax.fori_loop(1, ngraph, one, 0)
         tab[pl.ds(pl.multiple_of(hub_base + g * per, per), per)] = select_rows(tab, idx_ref[g, nsend:])
 
+    def wait_halo(tab, layer):
         def arrive(r, carry):
             for copy in halo_copies(tab, layer, r):
                 copy.wait_recv()
@@ -173,17 +174,34 @@
 
     inv = inv_ref[...]
 
-    def block(tab, rb):
-        a = a_v[pl.ds(pl.multiple_of(rb * DB, DB), DB), :]
-        out = jnp.dot(jnp.concatenate(bf16_parts(a), axis=0), tab[...], preferred_element_type=F32)
-        return (out[:DB] + (out[DB:2 * DB] + out[2 * DB:])) * inv
+    def chunk(i):
+        return pl.ds(pl.multiple_of(i * DB, DB), DB)
+
+    def product(a, tab):
+        out = jnp.dot(jnp.concatenate(bf16_parts(a), axis=0), tab, preferred_element_type=F32)
+        return out[:DB] + (out[DB:2 * DB] + out[2 * DB:])
+
+    def a_copy(rb):
+        return pltpu.make_async_copy(a_hbm.at[chunk(rb)], a_v.at[chunk(rb)], a_sem.at[rb])
+
+    def own_part(tab, layer):
+        def one(rb, carry):
+            if layer == 0:
+                a_copy(rb).wait()
+            acc[chunk(rb)] = product(a_v[chunk(rb), :vert], tab[:vert])
+            return carry
+
+        lax.fori_loop(0, nblock + 1, one, 0)
+
+    def far_part(tab, rb):
+        return (acc[chunk(rb)] + product(a_v[chunk(rb), vert:], tab[vert:])) * inv
 
     def hub_copy(layer, r):
         p = gpeer(r)
         return grdma(hubsend.at[layer, pl.ds(pl.multiple_of(p * per, per), per)], hubrecv.at[layer, g], us.at[layer, r - 1], ur.at[layer, r - 1], r)
 
     def exchange_hubs(tab, layer):
-        hubsend[layer] = block(tab, nblock)
+        hubsend[layer] = far_part(tab, nblock)
         for r in range(1, ngraph):
             hub_copy(layer, r).start()
         hubrecv[layer, g] = hubsend[layer, pl.ds(pl.multiple_of(g * per, per), per)]
@@ -195,23 +213,19 @@
         for p in range(1, ngraph):
             total = total + hubrecv[layer, p]
         fill = jnp.zeros((DB - 3 * per, total.shape[1]), BF16)
-        return jnp.concatenate([*bf16_parts(total), fill], axis=0)
-
-    def with_hubs(layer, totals, y, rb):
+        tot[layer] = jnp.concatenate([*bf16_parts(total), fill], axis=0)
+
+    def with_hubs(layer, rb):
         rows = lax.broadcasted_iota(jnp.int32, (DB, DB), 0) + rb * DB
         sel = jnp.where(rows == myhub_ref[...], F32(1), F32(0)).astype(BF16)
-        return y + jnp.dot(sel, totals, preferred_element_type=F32)
-
-    exchange_halo(tab1, 0)
-    for copy in a_copies:
-        copy.wait()
+        return acc[chunk(rb)] + jnp.dot(sel, tot[layer], preferred_element_type=F32)
+
+    start_halo(tab1, 0)
+    own_part(tab1, 0)
+    wait_halo(tab1, 0)
     exchange_hubs(tab1, 0)
-    totals1 = hub_totals(0)
     for copy in w2_copies:
         copy.wait_recv()
-
-    def chunk(i):
-        return pl.ds(pl.multiple_of(i * DB, DB), DB)
 
     def h_copy(i, r):
         return frdma(hsend.at[fpeer(r), chunk(i)], hin.at[f, chunk(i)], ns.at[i, r - 1], nr.at[i, r - 1], r)
@@ -238,43 +252,69 @@
 
     bias1 = b1_ref[...]
 
-    def rows1(t, carry):
+    def place(t):
         i, rr = t // nfeat, lax.rem(t, nfeat)
         q = fpeer(rr + 1)
-        rb = q * nchunk + i
-        h = jnp.maximum(with_hubs(0, totals1, block(tab1, rb), rb) + bias1, 0.0).astype(BF16)
-
-        @pl.when(rr < nfeat - 1)
-        def _():
-            hsend[q, chunk(i)] = h
-            h_copy(i, rr + 1).start()
-
-        @pl.when(rr == nfeat - 1)
-        def _():
-            hin[f, chunk(i)] = h
-
-        @pl.when((rr == nfeat - 2) & (i > 0))
-        def _():
-            z2_chunk(i - 1)
+        return i, rr, q, q * nchunk + i
+
+    def rows1(t, carry):
+        @pl.when(t < nblock)
+        def _():
+            rb = place(t)[3]
+            acc[chunk(rb)] = far_part(tab1, rb)
+
+        @pl.when(t == LAG)
+        def _():
+            hub_totals(0)
+
+        @pl.when(t >= LAG)
+        def _():
+            i, rr, q, rb = place(t - LAG)
+            h = jnp.maximum(with_hubs(0, rb) + bias1, 0.0).astype(BF16)
+
+            @pl.when(rr < nfeat - 1)
+            def _():
+                hsend[q, chunk(i)] = h
+                h_copy(i, rr + 1).start()
+
+            @pl.when(rr == nfeat - 1)
+            def _():
+                hin[f, chunk(i)] = h
+
+            @pl.when((rr == nfeat - 2) & (i > 0))
+            def _():
+                z2_chunk(i - 1)
 
         return carry
 
-    lax.fori_loop(0, nblock, rows1, 0)
+    lax.fori_loop(0, nblock + LAG, rows1, 0)
     z2_chunk(nchunk - 1)
     for i in range(nchunk):
         for r in range(1, nfeat):
             z2_copy(i, r).wait_recv()
 
-    exchange_halo(tab2, 1)
+    start_halo(tab2, 1)
+    own_part(tab2, 1)
+    wait_halo(tab2, 1)
     exchange_hubs(tab2, 1)
-    totals2 = hub_totals(1)
     bias2 = b2_ref[...]
 
-    def rows2(rb, carry):
-        o_ref[chunk(rb), :] = with_hubs(1, totals2, block(tab2, rb), rb) + bias2
+    def rows2(t, carry):
+        @pl.when(t < nblock)
+        def _():
+            acc[chunk(t)] = far_part(tab2, t)
+
+        @pl.when(t == LAG)
+        def _():
+            hub_totals(1)
+
+        @pl.when(t >= LAG)
+        def _():
+            o_ref[chunk(t - LAG), :] = with_hubs(1, t - LAG) + bias2
+
         return carry
 
-    lax.fori_loop(0, nblock, rows2, 0)
+    lax.fori_loop(0, nblock + LAG, rows2, 0)
 
     for copy in x_copies + w1_copies + w2_copies:
         copy.wait_send()
@@ -303,7 +343,7 @@
         in_specs=[vspec] * 8 + [pl.BlockSpec(memory_space=pl.ANY)],
         out_specs=vspec,
         scratch_shapes=[
-            vm(adj.shape, F32), vm((nfeat, part, x.shape[1]), BF16), vm((nfeat, *w1.shape), BF16), vm((nfeat, *w2.shape), BF16),
+            vm(adj.shape, F32), vm((adj.shape[0], cols), F32), vm((2, DB, cols), BF16), vm((nfeat, part, x.shape[1]), BF16), vm((nfeat, *w1.shape), BF16), vm((nfeat, *w2.shape), BF16),
             vm((adj.shape[1], cols), BF16), vm((adj.shape[1], cols), BF16), vm((nfeat, part, cols), BF16), vm((nfeat, part, cols), BF16),
             vm((nfeat, part, cols), BF16), vm((2, ngraph, nsend + per, cols), BF16), vm((2, ngraph * per, cols), F32), vm((2, ngraph, per, cols), F32),
             dma(nblk), dma(fr), dma(fr), dma(fr), dma(fr), dma(fr), dma(fr), dma(fr), dma(fr), dma(nchunk, fr), dma(nchunk, fr),

time: 176 us -> 174 us (0.989)
  Pallas kernels: 137 us -> 134 us
    pallas_call x1, Pallas kernels: 107 us -> 105 us  [run_layers(): pl.pallas_call(functools.partial(layers_kernel, (nfeat, ngraph, vert, nse...]
where the time goes in v1:
time: 174 us; the launch traced here: 173 us
  Pallas kernels  134 us (77%)
  other arithmetic  31.2 us (18%)
  local copies, waits for them, and re-layouts  7.2 us (4%)
    pallas_call x1, Pallas kernels, run_layers(): pl.pallas_call(functools.partial(layers_kernel, (nfeat, ngraph, vert, nse...  105 us
    pallas_call x1, Pallas kernels, build_adjacency(): pl.pallas_call(functools.partial(build_kernel, nsb), out_shape=jax.ShapeD...  29.3 us
    sort x1, other arithmetic, device_program(): skey, sw = lax.sort((key, coef), num_keys=1, is_stable=False)  18.4 us
    reduce_sum x1, other arithmetic, device_program(): starts = jnp.sum((key[None, :] < bound[:, None]).astype(jnp.int32), axis=1)  6.46 us

profile of v1, /device:TPU:97, one launch (start us, length us, event | category | flops | bytes accessed | tf_op | source)
XLA Modules:
  0.0 173.2 jit_solution(5188375581380506050)
XLA Ops:
  0.0 1.6 fusion.15
  2.3 1.0 broadcast_multiply_fusion
  3.3 1.4 fusion.4
  4.7 0.0 copy-start.3
  4.7 18.4 %sort.15 = (s32[40960]{0:T(1024)S(1)}, f32[40960]{0:T(1024)S(1)}) sort(s32[40960]{0:T(1024)S(1)} %fusion.4, f32[40960]{0:T(1024)S(1)} %broadcast_multiply_fusion), dimensions={0}, to_apply=%region_4.5 | sort | flops 655360 | bytes 655360 | tf_op jit(solution)/shard_map/sort | solution.py:391
  23.2 0.1 add_convert_fusion.1
  23.2 1.7 select_maximum_fusion.edges_ref
  25.0 0.0 copy-done.3
  25.0 0.2 convert_reduce_fusion.1
  25.2 0.1 select_reduce_fusion
  25.3 0.8 broadcast_in_dim.80.rowid_ref
  26.1 0.8 broadcast_in_dim.81.colid_ref
  26.9 6.5 %convert_reduce_fusion.starts_ref = s32[290]{0:T(512)} fusion(s32[40960]{0:T(1024)S(1)} %fusion.4, s32[290]{0:T(512)S(1)} %fusion.22), kind=kLoop, calls=%fused_computation | loop fusion | flops 35634912 | bytes 166160 | tf_op jit(solution)/shard_map/reduce_sum | solution.py:390
  33.3 0.0 copy-start.1
  33.3 0.0 copy-start.2
  33.3 29.3 %build.1.a_hbm = f32[2176,4352]{1,0:T(8,128)} custom-call(s32[290]{0:T(512)} %convert_reduce_fusion.starts_ref, f32[8,41472]{1,0:T(8,128)} %select_maximum_fusion.edges_ref, bf16[2,128,256]{2,1,0:T(8,128)(2,1)} %broadcast_in_dim.80.rowid_ref, bf16[256,256]{1,0:T(8,128)(2,1)} %broadcast_in_dim.81.colid_ref), custom_call_target="tpu_custom_call" | custom-call | tf_op jit(solution)/shard_map/build/pallas_call | solution.py:59
  62.6 0.0 copy-start
  62.6 0.1 dynamic-slice_subtract_fusion
  62.7 0.0 copy-done.1
  62.7 0.0 copy-done.2
  62.7 1.3 broadcast_in_dim.74.idx_ref
  64.0 0.1 pad_add_fusion.1
  64.1 0.5 pad_bitcast_fusion.myhub_ref
  64.7 0.5 broadcast_in_dim.78.inv_ref
  65.1 0.0 copy-done
  65.1 1.0 copy.14.x_ref
  66.2 104.8 %layers.1 = f32[2048,128]{1,0:T(8,128)} custom-call(bf16[2048,75]{1,0:T(8,128)(2,1)} %copy.14.x_ref, bf16[75,512]{1,0:T(8,128)(2,1)} %w1_ref.1, bf16[128,512]{1,0:T(8,128)(2,1)} %w2_ref.1, s32[8,272,128]{2,1,0:T(8,128)} %broadcast_in_dim.74.idx_ref, s32[1,128]{1,0:T(1,128)} %pad_bitcast_fusion.myhub_ref, f32[1,128]{1,0:T(1,128)} %bitcast.12, ...), custom_call_target="tpu_custom_call" | custom-call | tf_op jit(solution)/shard_map/layers/pallas_call | solution.py:340
  171.0 2.3 %copy.16 = f32[2048,128]{1,0:T(8,128)} copy(f32[2048,128]{1,0:T(8,128)} %layers.1) | data formatting | bytes 2097152
  (10 shorter events, 0.1 us)
Async XLA Ops:
  4.7 20.2 %copy-start.3 = (s32[128]{0:T(128)S(1)}, s32[128]{0:T(128)}, u32[]{:S(2)}) copy-start(s32[128]{0:T(128)} %param.19) | copy-start | bytes 1540
  33.3 29.4 %copy-start.1 = (s32[8,256]{1,0:T(8,128)S(1)}, s32[8,256]{1,0:T(8,128)}, u32[]{:S(2)}) copy-start(s32[8,256]{1,0:T(8,128)} %param.17) | copy-start | bytes 24580
  33.3 29.4 %copy-start.2 = (s32[8,256]{1,0:T(8,128)S(1)}, s32[8,256]{1,0:T(8,128)}, u32[]{:S(2)}) copy-start(s32[8,256]{1,0:T(8,128)} %param.18) | copy-start | bytes 24580
  62.6 2.6 %copy-start = (bf16[2048,75]{0,1:T(8,128)(2,1)S(1)}, bf16[2048,75]{0,1:T(8,128)(2,1)}, u32[]{:S(2)}) copy-start(bf16[2048,75]{0,1:T(8,128)(2,1)} %param.12) | copy-start | bytes 921604

commit v2 on v1

--- a/solution.py
+++ b/solution.py
@@ -21,32 +21,37 @@
     return hi, mid, low
 
 
-def build_kernel(nsb, starts_ref, edges_ref, rowid_ref, colid_ref, a_ref):
+def build_kernel(ndb, nsb, starts_ref, edges_ref, hubcol_ref, a_ref):
     db = pl.program_id(0)
     dbase = (db * DB).astype(F32)
-    row_id = rowid_ref[0]
+    hub_col = hubcol_ref[...]
+    row_id = jnp.where(db == ndb - 1, hub_col, lax.broadcasted_iota(jnp.int32, (DB, 128), 0).astype(F32)).astype(BF16)
+    row_id = jnp.concatenate([row_id] * (KW // 128), axis=1)
     iota_s = lax.broadcasted_iota(jnp.int32, (SB, KW), 0).astype(BF16)
+    last_id = jnp.concatenate([hub_col, jnp.full((SB - DB, 128), 300.0, F32)], axis=0).astype(BF16)
+    last_id = jnp.concatenate([last_id] * (KW // 128), axis=1)
     zero = jnp.zeros((), BF16)
 
     def window(sb, start):
-        base = pl.multiple_of((start // 128) * 128, 128)
-        shift = start - base
-        raw = edges_ref[:, pl.ds(base, KW + 128)]
+        chunk = start // 128
+        shift = start - chunk * 128
+        raw = edges_ref[pl.ds(pl.multiple_of(chunk * 8, 8), 8 * (KW // 128 + 1)), :]
+        raw = jnp.concatenate([raw[8 * i:8 * i + 8] for i in range(KW // 128 + 1)], axis=1)
         rows = pltpu.roll(raw, KW + 128 - shift, 1)[:, :KW]
         dst = (rows[0:1] - dbase).astype(BF16)
         src = (rows[1:2] - F32(SB * sb)).astype(BF16)
         hit = row_id == dst
         d3 = jnp.concatenate([jnp.where(hit, part, zero) for part in bf16_parts(rows[2:3])], axis=0)
-        col_id = colid_ref[...] if sb == nsb - 1 else iota_s
+        col_id = last_id if sb == nsb - 1 else iota_s
         sel = jnp.where(col_id == src, jnp.ones((), BF16), zero)
         out = lax.dot_general(d3, sel, (((1,), (1,)), ((), ())), preferred_element_type=F32)
         return out[:DB] + (out[DB:2 * DB] + out[2 * DB:])
 
     for sb in range(nsb):
-        a_ref[:, sb * SB:(sb + 1) * SB] = window(sb, starts_ref[db * nsb + sb])
+        a_ref[:, sb * SB:(sb + 1) * SB] = window(sb, starts_ref[0, db * nsb + sb])
     for sb in range(nsb):
-        start = starts_ref[db * nsb + sb]
-        end = starts_ref[db * nsb + sb + 1]
+        start = starts_ref[0, db * nsb + sb]
+        end = starts_ref[0, db * nsb + sb + 1]
 
         def more(i, carry):
             a_ref[:, sb * SB:(sb + 1) * SB] += window(sb, start + i * KW)
@@ -55,75 +60,152 @@
         lax.fori_loop(1, (end - start + KW - 1) // KW, more, 0)
 
 
-def build_adjacency(starts, edges, rowid, colid, ndb, nsb):
+def build_adjacency(starts, edges, hub_col, ndb, nsb):
     return pl.pallas_call(
-        functools.partial(build_kernel, nsb),
+        functools.partial(build_kernel, ndb, nsb),
         out_shape=jax.ShapeDtypeStruct((ndb * DB, nsb * SB), F32),
         grid_spec=pltpu.PrefetchScalarGridSpec(
             num_scalar_prefetch=1,
             grid=(ndb,),
-            in_specs=[
-                pl.BlockSpec(edges.shape, lambda i, s: (0, 0)),
-                pl.BlockSpec((1, DB, KW), lambda i, s: (i // (ndb - 1), 0, 0)),
-                pl.BlockSpec(colid.shape, lambda i, s: (0, 0)),
-            ],
+            in_specs=[pl.BlockSpec(edges.shape, lambda i, s: (0, 0)), pl.BlockSpec(hub_col.shape, lambda i, s: (0, 0))],
             out_specs=pl.BlockSpec((DB, nsb * SB), lambda i, s: (i, 0)),
         ),
         name="build",
-    )(starts, edges, rowid, colid)
-
-
-def layers_kernel(dims, x_ref, w1_ref, w2_ref, idx_ref, myhub_ref, b1_ref, b2_ref, inv_ref, a_hbm, o_ref,
-                  a_v, acc, tot, xin, w1in, w2in, tab1, tab2, zout, hsend, hin, halo, hubsend, hubrecv,
-                  a_sem, xs, xr, w1s, w1r, w2s, w2r, z1s, z1r, z2s, z2r, hs, hr, ps, pr, us, ur, ns, nr):
-    nfeat, ngraph, vert, nsend, per = dims
-    part, rows_send = vert // nfeat, nsend + per
-    nchunk = part // DB
-    f, g = lax.axis_index("feat"), lax.axis_index("graph")
-    halo_base, hub_base = vert, vert + ngraph * nsend
-    nblock = vert // DB
+    )(starts, edges, hub_col)
+
+
+def iota2(axis):
+    return lax.broadcasted_iota(jnp.int32, (8, 128), axis)
+
+
+def sort_levels(kref, wref, first, last):
+    sub, lane = iota2(0), iota2(1)
+
+    def bit(b):
+        return ((sub >> (b - 6)) & 1) == 1 if b < 9 else ((lane >> (b - 9)) & 1) == 1
+
+    def within(level):
+        steps = []
+        for j in range(level - 1, 5, -1):
+            high = bit(j)
+            if level < 16:
+                want_max = high != bit(level)
+            else:
+                want_max = high
+            steps.append((j, high, want_max))
+
+        def body(it, carry):
+            pairs = [(kref[it * 16 + u], wref[it * 16 + u]) for u in range(16)]
+            for j, high, want_max in steps:
+                axis, m, size = (0, 1 << (j - 6), 8) if j < 9 else (1, 1 << (j - 9), 128)
+                new = []
+                index = (lane if axis else sub) ^ m
+                for key, w in pairs:
+                    if 2 * m == size:
+                        pk, pw = pltpu.roll(key, m, axis), pltpu.roll(w, m, axis)
+                    else:
+                        pk = jnp.take_along_axis(key, index, axis=axis)
+                        pw = jnp.take_along_axis(w, index, axis=axis)
+                    nk = jnp.where(want_max, jnp.maximum(key, pk), jnp.minimum(key, pk))
+                    new.append((nk, jnp.where(nk == key, w, pw)))
+                pairs = new
+            for u, (key, w) in enumerate(pairs):
+                kref[it * 16 + u] = key
+                wref[it * 16 + u] = w
+            return carry
+
+        lax.fori_loop(0, 4, body, 0)
+
+    def across(level, top, low):
+        base = 3 if low >= 3 else 0
+
+        def body(it, carry):
+            where_v = [(it + 8 * u) if base == 3 else (it * 8 + u) for u in range(8)]
+            ks, ws = [kref[v] for v in where_v], [wref[v] for v in where_v]
+            for j in range(top, low - 1, -1):
+                m = 1 << (j - base)
+                for u in range(8):
+                    if u & m:
+                        continue
+                    a, b = u, u | m
+                    down = None
+                    if level < 6 and base <= level < base + 3:
+                        flip = bool(u >> (level - base) & 1)
+                        swap = (ks[a] < ks[b]) if flip else (ks[a] > ks[b])
+                    elif level < 6:
+                        down = jnp.full((8, 128), (it >> (level - 3 + base)) & 1, jnp.int32) == 1
+                        swap = (ks[a] > ks[b]) != down
+                    elif level < 16:
+                        swap = (ks[a] > ks[b]) != bit(level)
+                    else:
+                        swap = ks[a] > ks[b]
+                    ks[a], ks[b] = jnp.where(swap, ks[b], ks[a]), jnp.where(swap, ks[a], ks[b])
+                    ws[a], ws[b] = jnp.where(swap, ws[b], ws[a]), jnp.where(swap, ws[a], ws[b])
+            for u, v in enumerate(where_v):
+                kref[v] = ks[u]
+                wref[v] = ws[u]
+            return carry
+
+        lax.fori_loop(0, 8, body, 0)
+
+    for level in range(first, last + 1):
+        if level > 6:
+            within(level)
+        if level > 3:
+            across(level, min(level - 1, 5), 3)
+        across(level, min(level - 1, 2), 0)
+
+
+def pre_kernel(dims, dst_ref, src_ref, valid_ref, w_ref, x_ref, w1_ref, w2_ref,
+               edges_ref, starts_ref, tab_ref, w2all_ref, inv_ref,
+               kref, wref, xin, w1in, w2in, tab, zout, xs, xr, w1s, w1r, w2s, w2r, zs, zr):
+    nfeat, ngraph, ndb, nsb = dims
+    vert = x_ref.shape[0]
+    part = vert // nfeat
+    f = lax.axis_index("feat")
 
     def fpeer(r):
         return lax.rem(f + r, nfeat)
 
-    def gpeer(r):
-        return lax.rem(g + r, ngraph)
-
     def frdma(src, dst, send, recv, r):
         return pltpu.make_async_remote_copy(src, dst, send, recv, device_id={"feat": fpeer(r)}, device_id_type=MESH)
 
-    def grdma(src, dst, send, recv, r):
-        return pltpu.make_async_remote_copy(src, dst, send, recv, device_id={"graph": gpeer(r)}, device_id_type=MESH)
-
-    for i in range(a_hbm.shape[0] // DB):
-        pltpu.make_async_copy(a_hbm.at[pl.ds(i * DB, DB)], a_v.at[pl.ds(i * DB, DB)], a_sem.at[i]).start()
+    def quarter(q):
+        return pl.ds(pl.multiple_of(q * part, part), part)
 
     barrier = pltpu.get_barrier_semaphore()
     for r in range(1, nfeat):
         pl.semaphore_signal(barrier, inc=1, device_id={"feat": fpeer(r)}, device_id_type=MESH)
-    for r in range(1, ngraph):
-        pl.semaphore_signal(barrier, inc=1, device_id={"graph": gpeer(r)}, device_id_type=MESH)
-    pl.semaphore_wait(barrier, nfeat + ngraph - 2)
-
-    def quarter(q):
-        return pl.ds(pl.multiple_of(q * part, part), part)
-
-    x_copies = [frdma(x_ref.at[quarter(fpeer(r))], xin.at[f], xs.at[r - 1], xr.at[r - 1], r) for r in range(1, nfeat)]
-    w1_copies = [frdma(w1_ref, w1in.at[f], w1s.at[r - 1], w1r.at[r - 1], r) for r in range(1, nfeat)]
-    w2_copies = [frdma(w2_ref, w2in.at[f], w2s.at[r - 1], w2r.at[r - 1], r) for r in range(1, nfeat)]
-    for copy in w1_copies + x_copies + w2_copies:
+    pl.semaphore_wait(barrier, nfeat - 1)
+    peers = range(1, nfeat)
+    x_copies = [frdma(x_ref.at[quarter(fpeer(r))], xin.at[f], xs.at[r - 1], xr.at[r - 1], r) for r in peers]
+    w1_copies = [frdma(w1_ref, w1in.at[f], w1s.at[r - 1], w1r.at[r - 1], r) for r in peers]
+    w2_copies = [frdma(w2_ref, w2in.at[f], w2s.at[r - 1], w2r.at[r - 1], r) for r in peers]
+    z_copies = [frdma(zout.at[fpeer(r)], tab.at[quarter(f)], zs.at[r - 1], zr.at[r - 1], r) for r in peers]
+    for copy in w1_copies + x_copies:
         copy.start()
     xin[f] = x_ref[quarter(f)]
     w1in[f] = w1_ref[...]
     w2in[f] = w2_ref[...]
-    pad_rows = a_v.shape[1] - hub_base - ngraph * per
-    for tab in (tab1, tab2):
-        tab[pl.ds(pl.multiple_of(halo_base + g * nsend, nsend), nsend)] = jnp.zeros((nsend, tab.shape[1]), BF16)
-        tab[hub_base + ngraph * per:] = jnp.zeros((pad_rows, tab.shape[1]), BF16)
+
+    dst, src = dst_ref[...], src_ref[...]
+    key = (((dst // DB) * nsb + src // SB) << 15) | ((dst % DB) << 8) | (src % SB)
+    nbucket = ndb * nsb
+    key = jnp.where(valid_ref[...] > 0, key, nbucket << 15).astype(F32)
+    coef = w_ref[...] * valid_ref[...].astype(F32)
+    large = jnp.max(coef, keepdims=True) > 1e30
+    coef = coef * jnp.where(large, F32(2.0**-40), F32(1))
+    inv_ref[...] = jnp.broadcast_to(jnp.where(large, F32(2.0**40), F32(1)), inv_ref.shape)
+    used = dst.shape[0] // 8
+    kref[:used] = key.reshape(used, 8, 128)
+    wref[:used] = coef.reshape(used, 8, 128)
+    kref[used:] = jnp.full((64 - used, 8, 128), nbucket << 15, F32)
+    wref[used:] = jnp.zeros((64 - used, 8, 128), F32)
+    sort_levels(kref, wref, 1, 11)
 
     for copy in w1_copies + x_copies:
         copy.wait_recv()
-    cols = tab1.shape[1]
+    cols = tab.shape[1]
     z = None
     for s in range(nfeat):
         term = jnp.dot(xin[s], w1in[s], preferred_element_type=F32)
@@ -131,12 +213,109 @@
     z = z.astype(BF16)
     for q in range(nfeat):
         zout[q] = z[:, q * cols:(q + 1) * cols]
-    z1_copies = [frdma(zout.at[fpeer(r)], tab1.at[quarter(f)], z1s.at[r - 1], z1r.at[r - 1], r) for r in range(1, nfeat)]
-    for copy in z1_copies:
+    for copy in z_copies + w2_copies:
         copy.start()
-    tab1[quarter(f)] = zout[f]
-    for copy in z1_copies:
+    tab[quarter(f)] = zout[f]
+    sort_levels(kref, wref, 12, 16)
+
+    nb = starts_ref.shape[1]
+    bound = (lax.broadcasted_iota(jnp.int32, (nb, 1), 0) << 15).astype(F32)
+    last = kref[63, 7:8, :]
+    lane = lax.broadcasted_iota(jnp.int32, (1, 128), 1)
+    before = jnp.where(lane == 0, F32(-1), pltpu.roll(last, 1, 1))
+    full = last < bound
+    row_sel = jnp.where((before < bound) & jnp.logical_not(full), F32(1), F32(0)).astype(BF16)
+    keys = kref[...].reshape(512, 128)
+    picked = None
+    for piece in bf16_parts(keys):
+        term = lax.dot_general(row_sel, piece, (((1,), (1,)), ((), ())), preferred_element_type=F32)
+        picked = term if picked is None else picked + term
+    inside = jnp.where(picked < bound, F32(1), F32(0)).astype(BF16)
+    count = lax.dot_general(jnp.ones((8, 512), BF16), inside, (((1,), (1,)), ((), ())), preferred_element_type=F32)
+    rows = lax.dot_general(jnp.ones((8, 128), BF16), jnp.where(full, F32(1), F32(0)).astype(BF16), (((1,), (1,)), ((), ())), preferred_element_type=F32)
+    starts_ref[...] = (count + 512.0 * rows).astype(jnp.int32)
+
+    nl = edges_ref.shape[0] // 32
+    for k in range(4):
+        kk = jnp.concatenate([kref[:, 2 * k, :], kref[:, 2 * k + 1, :]], axis=0)
+        ww = jnp.concatenate([wref[:, 2 * k, :], wref[:, 2 * k + 1, :]], axis=0)
+        ki = kk.astype(jnp.int32)
+        bucket = ki >> 15
+        block = jnp.floor((bucket.astype(F32) + 0.5) * F32(1.0 / nsb))
+        edge_dst = block * DB + ((ki >> 8) & (DB - 1)).astype(F32)
+        edge_src = (bucket.astype(F32) - block * nsb) * SB + (ki & (SB - 1)).astype(F32)
+        for field, val in enumerate((edge_dst, edge_src, ww)):
+            edges_ref[pl.ds(k * 8 + field, nl, stride=32), :] = val.T[:nl]
+
+    for copy in z_copies + w2_copies:
         copy.wait_recv()
+    tab_ref[...] = tab[...]
+    w2all_ref[...] = w2in[...]
+    for copy in x_copies + w1_copies + w2_copies + z_copies:
+        copy.wait_send()
+
+
+def run_pre(nfeat, ngraph, ndb, nsb, dst, src, valid, w, x, w1, w2):
+    vert, part = x.shape[0], x.shape[0] // nfeat
+    cols = w1.shape[1] // nfeat
+    nrows = dst.shape[0]
+    vm = lambda shape, dt: pltpu.VMEM(shape, dt)
+    dma = pltpu.SemaphoreType.DMA((nfeat - 1,))
+    vspec = pl.BlockSpec(memory_space=pltpu.VMEM)
+    shape = jax.ShapeDtypeStruct
+    return pl.pallas_call(
+        functools.partial(pre_kernel, (nfeat, ngraph, ndb, nsb)),
+        out_shape=[shape(((nrows + 4) * 8, 128), F32), shape((8, 384), jnp.int32), shape((vert, cols), BF16), shape((nfeat, *w2.shape), BF16), shape((1, cols), F32)],
+        in_specs=[vspec] * 7,
+        out_specs=[vspec] * 5,
+        scratch_shapes=[
+            vm((64, 8, 128), F32), vm((64, 8, 128), F32), vm((nfeat, part, x.shape[1]), BF16), vm((nfeat, *w1.shape), BF16), vm((nfeat, *w2.shape), BF16),
+            vm((vert, cols), BF16), vm((nfeat, part, cols), BF16), dma, dma, dma, dma, dma, dma, dma, dma,
+        ],
+        compiler_params=pltpu.CompilerParams(collective_id=0, has_side_effects=True, vmem_limit_bytes=40 * 2**20),
+        name="pre",
+    )(dst, src, valid, w, x, w1, w2)
+
+
+def layers_kernel(dims, tabown_ref, w2in, idx_ref, myhub_ref, b1_ref, b2_ref, inv_ref, a_hbm, o_ref,
+                  a_v, acc, tot, tab1, tab2, zout, hsend, hin, halo, hubsend, hubrecv,
+                  a_sem, z2s, z2r, hs, hr, ps, pr, us, ur, ns, nr):
+    nfeat, ngraph, vert, nsend, per = dims
+    part, rows_send = vert // nfeat, nsend + per
+    nchunk = part // DB
+    f, g = lax.axis_index("feat"), lax.axis_index("graph")
+    halo_base, hub_base = vert, vert + ngraph * nsend
+    nblock = vert // DB
+
+    def fpeer(r):
+        return lax.rem(f + r, nfeat)
+
+    def gpeer(r):
+        return lax.rem(g + r, ngraph)
+
+    def frdma(src, dst, send, recv, r):
+        return pltpu.make_async_remote_copy(src, dst, send, recv, device_id={"feat": fpeer(r)}, device_id_type=MESH)
+
+    def grdma(src, dst, send, recv, r):
+        return pltpu.make_async_remote_copy(src, dst, send, recv, device_id={"graph": gpeer(r)}, device_id_type=MESH)
+
+    for i in range(a_hbm.shape[0] // DB):
+        pltpu.make_async_copy(a_hbm.at[pl.ds(i * DB, DB)], a_v.at[pl.ds(i * DB, DB)], a_sem.at[i]).start()
+
+    barrier = pltpu.get_barrier_semaphore()
+    for r in range(1, nfeat):
+        pl.semaphore_signal(barrier, inc=1, device_id={"feat": fpeer(r)}, device_id_type=MESH)
+    for r in range(1, ngraph):
+        pl.semaphore_signal(barrier, inc=1, device_id={"graph": gpeer(r)}, device_id_type=MESH)
+    pl.semaphore_wait(barrier, nfeat + ngraph - 2)
+
+    pad_rows = a_v.shape[1] - hub_base - ngraph * per
+    for tab in (tab1, tab2):
+        tab[pl.ds(pl.multiple_of(halo_base + g * nsend, nsend), nsend)] = jnp.zeros((nsend, tab.shape[1]), BF16)
+        tab[hub_base + ngraph * per:] = jnp.zeros((pad_rows, tab.shape[1]), BF16)
+
+    cols = tab1.shape[1]
+    tab1[:vert] = tabown_ref[...]
 
     lane = lax.broadcasted_iota(jnp.int32, (1, DB), 1)
 
@@ -224,17 +403,11 @@
     own_part(tab1, 0)
     wait_halo(tab1, 0)
     exchange_hubs(tab1, 0)
-    for copy in w2_copies:
-        copy.wait_recv()
-
     def h_copy(i, r):
         return frdma(hsend.at[fpeer(r), chunk(i)], hin.at[f, chunk(i)], ns.at[i, r - 1], nr.at[i, r - 1], r)
 
     def z2_copy(i, r):
         return frdma(zout.at[fpeer(r), chunk(i)], tab2.at[pl.ds(pl.multiple_of(f * part + i * DB, DB), DB)], z2s.at[i, r - 1], z2r.at[i, r - 1], r)
-
-    for copy in z1_copies:
-        copy.wait_send()
 
     def z2_chunk(i):
         for r in range(1, nfeat):
@@ -316,8 +489,6 @@
 
     lax.fori_loop(0, nblock + LAG, rows2, 0)
 
-    for copy in x_copies + w1_copies + w2_copies:
-        copy.wait_send()
     for i in range(nchunk):
         for r in range(1, nfeat):
             h_copy(i, r).wait_send()
@@ -329,8 +500,8 @@
             hub_copy(layer, r).wait_send()
 
 
-def run_layers(nfeat, ngraph, nsend, per, x, w1, w2, idx, myhub, b1, b2, inv, adj):
-    vert = x.shape[0]
+def run_layers(nfeat, ngraph, nsend, per, tab_own, w2, idx, myhub, b1, b2, inv, adj):
+    vert = tab_own.shape[0]
     part, cols = vert // nfeat, b1.shape[1]
     nchunk, nblk = part // DB, adj.shape[0] // DB
     vm = lambda shape, dt: pltpu.VMEM(shape, dt)
@@ -340,18 +511,18 @@
     return pl.pallas_call(
         functools.partial(layers_kernel, (nfeat, ngraph, vert, nsend, per)),
         out_shape=jax.ShapeDtypeStruct((vert, cols), F32),
-        in_specs=[vspec] * 8 + [pl.BlockSpec(memory_space=pl.ANY)],
+        in_specs=[vspec] * 7 + [pl.BlockSpec(memory_space=pl.ANY)],
         out_specs=vspec,
         scratch_shapes=[
-            vm(adj.shape, F32), vm((adj.shape[0], cols), F32), vm((2, DB, cols), BF16), vm((nfeat, part, x.shape[1]), BF16), vm((nfeat, *w1.shape), BF16), vm((nfeat, *w2.shape), BF16),
+            vm(adj.shape, F32), vm((adj.shape[0], cols), F32), vm((2, DB, cols), BF16),
             vm((adj.shape[1], cols), BF16), vm((adj.shape[1], cols), BF16), vm((nfeat, part, cols), BF16), vm((nfeat, part, cols), BF16),
             vm((nfeat, part, cols), BF16), vm((2, ngraph, nsend + per, cols), BF16), vm((2, ngraph * per, cols), F32), vm((2, ngraph, per, cols), F32),
-            dma(nblk), dma(fr), dma(fr), dma(fr), dma(fr), dma(fr), dma(fr), dma(fr), dma(fr), dma(nchunk, fr), dma(nchunk, fr),
+            dma(nblk), dma(nchunk, fr), dma(nchunk, fr),
             dma(2, gr), dma(2, gr), dma(2, gr), dma(2, gr), dma(2, gr), dma(2, gr), dma(nchunk, fr), dma(nchunk, fr),
         ],
-        compiler_params=pltpu.CompilerParams(collective_id=0, has_side_effects=True, vmem_limit_bytes=62 * 2**20),
+        compiler_params=pltpu.CompilerParams(collective_id=1, has_side_effects=True, vmem_limit_bytes=62 * 2**20),
         name="layers",
-    )(x, w1, w2, idx, myhub, b1, b2, inv, adj)
+    )(tab_own, w2, idx, myhub, b1, b2, inv, adj)
 
 
 def solution(mesh):
@@ -364,7 +535,6 @@
         nhub = hub_ids.shape[0]
         per = nhub // ngraph
         nsend = send_loc.shape[1]
-        cols = b_first.shape[0]
         me = lax.axis_index("graph")
         ndb = (vert + nhub) // DB
         table_rows = vert + ngraph * nsend + nhub
@@ -379,32 +549,16 @@
         k_by_pos = jnp.sum(jnp.where(at_pos, ks[None, :], 0), axis=1)
         my_hubs = lax.dynamic_slice(hub_by_pos, (me * per,), (per,)) - me * vert
 
-        key = ((dst_loc // DB) << 20) | ((src_loc // SB) << 15) | ((dst_loc % DB) << 8) | (src_loc % SB)
-        key = jnp.where(valid_loc > 0, key, 1 << 26)
-        coef = w_loc * valid_loc.astype(F32)
-        large = jnp.max(coef) > 1e30
-        coef = coef * jnp.where(large, F32(2.0**-40), F32(1))
-        inv = jnp.where(large, F32(2.0**40), F32(1))
-        nb = jnp.arange(ndb * nsb + 1)
-        bound = ((nb // nsb) << 20) | ((nb % nsb) << 15)
-        starts = jnp.sum((key[None, :] < bound[:, None]).astype(jnp.int32), axis=1)
-        skey, sw = lax.sort((key, coef), num_keys=1, is_stable=False)
-        sdst = (skey >> 20) * DB + ((skey >> 8) & (DB - 1))
-        ssrc = ((skey >> 15) & 31) * SB + (skey & (SB - 1))
-        edges = jnp.stack([sdst.astype(F32), ssrc.astype(F32), sw])
-        edges = jnp.pad(edges, ((0, 5), (0, 2 * KW)), constant_values=-1.0)
-        rowid = jnp.stack([jnp.arange(DB), k_by_pos]).astype(BF16)
-        rowid = jnp.broadcast_to(rowid[:, :, None], (2, DB, KW))
-        colid = jnp.pad(k_by_pos, (0, SB - nhub), constant_values=300).astype(BF16)
-        colid = jnp.broadcast_to(colid[:, None], (SB, KW))
-        adj = build_adjacency(starts, edges, rowid, colid, ndb, nsb)
+        grid = lambda v: v.reshape(-1, 128)
+        edges, starts, tab_own, w2_all, inv = run_pre(nfeat, ngraph, ndb, nsb, grid(dst_loc), grid(src_loc), grid(valid_loc), grid(w_loc), x_loc, w_first, w_second)
+        hub_col = jnp.broadcast_to(k_by_pos.astype(F32)[:, None], (DB, 128))
+        adj = build_adjacency(starts, edges, hub_col, ndb, nsb)
 
         idx = jnp.where(keep_loc > 0, send_loc, -1)
         idx = jnp.concatenate([idx, jnp.broadcast_to(my_hubs[None, :], (ngraph, per))], axis=1)
         idx = jnp.broadcast_to(idx[:, :, None], (*idx.shape, DB))
         myhub = jnp.pad(jnp.concatenate([my_hubs] * 3), (0, DB - 3 * per), constant_values=-1)[None, :]
-        inv = jnp.full((1, cols), inv)
-        return run_layers(nfeat, ngraph, nsend, per, x_loc, w_first, w_second, idx, myhub, b_first[None, :], b_second[None, :], inv, adj)
+        return run_layers(nfeat, ngraph, nsend, per, tab_own, w2_all, idx, myhub, b_first[None, :], b_second[None, :], inv, adj)
 
     edge_spec = P(rows_axes)
     send_spec = P(rows_axes, None)

time: 174 us -> 152 us (0.87)
  other arithmetic: 31.2 us -> 3.22 us
  Pallas kernels: 134 us -> 137 us
  local copies, waits for them, and re-layouts: 7.2 us -> 9.96 us
    pallas_call x1 -> x2, Pallas kernels: 29.3 us -> 64.2 us  [the longest x1 35.3 us: build_adjacency(): pl.pallas_call(functools.partial(build_kernel, ndb, nsb), out_shape=jax.S...]
    pallas_call x1, Pallas kernels: 105 us -> 73.2 us  [run_layers(): pl.pallas_call(functools.partial(layers_kernel, (nfeat, ngraph, vert, nse...]
    sort x1 -> x0, other arithmetic: 18.4 us -> none  [device_program(): skey, sw = lax.sort((key, coef), num_keys=1, is_stable=False)]
    reduce_sum x1 -> x0, other arithmetic: 6.46 us -> none  [device_program(): starts = jnp.sum((key[None, :] < bound[:, None]).astype(jnp.int32), axis=1)]
    unnamed x10 -> x24, local copies, waits for them, and re-layouts: 3.31 us -> 7.38 us
    another operation x4 -> x0, other arithmetic: 1.75 us -> none  [the longest x1 1.73 us: device_program(): edges = jnp.stack([sdst.astype(F32), ssrc.astype(F32), sw])]
where the time goes in v2:
time: 152 us; the launch traced here: 151 us
  Pallas kernels  137 us (90%)
  local copies, waits for them, and re-layouts  9.96 us (7%)
  other arithmetic  3.22 us (2%)
    pallas_call x1, Pallas kernels, run_layers(): pl.pallas_call(functools.partial(layers_kernel, (nfeat, ngraph, vert, nse...  73.2 us
    pallas_call x1, Pallas kernels, build_adjacency(): pl.pallas_call(functools.partial(build_kernel, ndb, nsb), out_shape=jax.S...  35.3 us
    pallas_call x1, Pallas kernels, run_pre(): pl.pallas_call(functools.partial(pre_kernel, (nfeat, ngraph, ndb, nsb)),...  28.9 us
    unnamed x24, local copies, waits for them, and re-layouts  7.38 us

profile of v2, /device:TPU:97, one launch (start us, length us, event | category | flops | bytes accessed | tf_op | source)
XLA Modules:
  0.0 150.7 jit_solution(2691381389082642449)
XLA Ops:
  0.0 0.0 copy-start.7
  0.0 0.0 copy-start.8
  0.0 0.0 copy-start.6
  0.0 0.0 copy-start.5
  0.0 0.0 copy-start.4
  0.0 0.0 copy-start.3
  0.0 0.7 and_select_fusion
  0.8 0.2 convert_reduce_fusion
  1.0 0.7 multiply_add_fusion
  1.6 0.8 select_reduce_fusion
  2.4 0.1 dynamic-slice_subtract_fusion
  2.5 0.1 pad_add_fusion.1
  2.6 0.5 pad_bitcast_fusion.myhub_ref
  3.1 0.7 compare_select_fusion
  3.8 0.7 broadcast_in_dim.63.hubcol_ref
  4.5 1.3 copy.14.x_ref
  5.8 1.4 broadcast_in_dim.59.idx_ref
  7.1 0.0 copy-done.7
  7.1 0.0 copy-done.8
  7.1 0.0 copy-done.6
  7.1 0.0 copy-done.5
  7.1 0.0 copy-done.4
  7.2 0.0 copy-done.3
  7.2 28.9 %pre.1 = (f32[2592,128]{1,0:T(8,128)S(1)}, s32[8,384]{1,0:T(8,128)S(1)}, bf16[2048,128]{1,0:T(8,128)(2,1)S(1)}, bf16[4,128,512]{2,1,0:T(8,128)(2,1)S(1)}, f32[1,128]{1,0:T(1,128)S(1)}) custom-call(s32[320,128]{1,0:T(8,128)S(1)} %bitcast.8, s32[320,128]{1,0:T(8,128)S(1)} %bitcast.9, s32[320,128]{1,0:T(8,128)S(1)} %bitcast.10, f32[320,128]{1,0:T(8,128)S(1)} %bitcast.11, ...), custom_call_target="tpu_custom_call" | custom-call | tf_op jit(solution)/shard_map/pre/pallas_call | solution.py:266
  36.0 0.0 copy-start
  36.0 1.1 copy-done
  37.1 0.0 copy-start.1
  37.1 0.8 copy-done.1
  37.9 0.0 copy-start.2
  37.9 0.8 copy-done.2
  38.7 0.0 copy-start.9
  38.7 0.6 copy-done.9
  39.3 0.0 copy-start.10
  39.3 0.6 copy-done.10
  39.9 35.3 %build.1.a_hbm = f32[2176,4352]{1,0:T(8,128)} custom-call(s32[8,384]{1,0:T(8,128)} %copy-done.9, f32[2592,128]{1,0:T(8,128)} %copy-done, f32[128,128]{1,0:T(8,128)} %broadcast_in_dim.63.hubcol_ref), custom_call_target="tpu_custom_call" | custom-call | tf_op jit(solution)/shard_map/build/pallas_call | solution.py:64
  75.2 73.2 %layers.1 = f32[2048,128]{1,0:T(8,128)} custom-call(bf16[2048,128]{1,0:T(8,128)(2,1)} %copy-done.1, bf16[4,128,512]{2,1,0:T(8,128)(2,1)} %copy-done.2, s32[8,272,128]{2,1,0:T(8,128)} %broadcast_in_dim.59.idx_ref, s32[1,128]{1,0:T(1,128)} %pad_bitcast_fusion.myhub_ref, f32[1,128]{1,0:T(1,128)} %bitcast.12, f32[1,128]{1,0:T(1,128)} %bitcast.13, ...), custom_call_target="tpu_custom_call" | custom-call | tf_op jit(solution)/shard_map/layers/pallas_call | solution.py:511
  148.4 2.3 %copy.16 = f32[2048,128]{1,0:T(8,128)} copy(f32[2048,128]{1,0:T(8,128)} %layers.1) | data formatting | bytes 2097152
  (3 shorter events, 0.0 us)
Async XLA Ops:
  0.0 7.1 %copy-start.7 = (bf16[128,512]{1,0:T(8,128)(2,1)S(1)}, bf16[128,512]{1,0:T(8,128)(2,1)}, u32[]{:S(2)}) copy-start(bf16[128,512]{1,0:T(8,128)(2,1)} %w2_ref.1) | copy-start | bytes 393220
  0.0 7.1 %copy-start.8 = (bf16[75,512]{1,0:T(8,128)(2,1)S(1)}, bf16[75,512]{1,0:T(8,128)(2,1)}, u32[]{:S(2)}) copy-start(bf16[75,512]{1,0:T(8,128)(2,1)} %w1_ref.1) | copy-start | bytes 230404
  0.0 7.1 %copy-start.6 = (f32[40960]{0:T(1024)S(1)}, f32[40960]{0:T(1024)}, u32[]{:S(2)}) copy-start(f32[40960]{0:T(1024)} %param.16) | copy-start | bytes 491524
  0.0 7.1 %copy-start.5 = (s32[40960]{0:T(1024)S(1)}, s32[40960]{0:T(1024)}, u32[]{:S(2)}) copy-start(s32[40960]{0:T(1024)} %param.15) | copy-start | bytes 491524
  0.0 7.1 %copy-start.4 = (s32[40960]{0:T(1024)S(1)}, s32[40960]{0:T(1024)}, u32[]{:S(2)}) copy-start(s32[40960]{0:T(1024)} %param.14) | copy-start | bytes 491524
  0.0 7.1 %copy-start.3 = (s32[40960]{0:T(1024)S(1)}, s32[40960]{0:T(1024)}, u32[]{:S(2)}) copy-start(s32[40960]{0:T(1024)} %param.13) | copy-start | bytes 491524
  36.0 1.1 copy-start
  37.1 0.8 copy-start.1
  37.9 0.8 copy-start.2
  38.7 0.6 copy-start.9
  39.3 0.6 copy-start.10

commit v3 on v2

--- a/solution.py
+++ b/solution.py
@@ -8,7 +8,6 @@
 from jax.sharding import PartitionSpec as P
 
 DB, SB, KW = 128, 256, 256
-LAG = 4
 MESH = pl.DeviceIdType.MESH
 F32, BF16 = jnp.float32, jnp.bfloat16
 
@@ -21,54 +20,63 @@
     return hi, mid, low
 
 
-def build_kernel(ndb, nsb, starts_ref, edges_ref, hubcol_ref, a_ref):
+def build_kernel(ndb, nsb, ncol, starts_ref, edges_ref, hubcol_ref, a_ref):
     db = pl.program_id(0)
     dbase = (db * DB).astype(F32)
     hub_col = hubcol_ref[...]
     row_id = jnp.where(db == ndb - 1, hub_col, lax.broadcasted_iota(jnp.int32, (DB, 128), 0).astype(F32)).astype(BF16)
-    row_id = jnp.concatenate([row_id] * (KW // 128), axis=1)
-    iota_s = lax.broadcasted_iota(jnp.int32, (SB, KW), 0).astype(BF16)
-    last_id = jnp.concatenate([hub_col, jnp.full((SB - DB, 128), 300.0, F32)], axis=0).astype(BF16)
-    last_id = jnp.concatenate([last_id] * (KW // 128), axis=1)
+    iota_s = lax.broadcasted_iota(jnp.int32, (SB, 128), 0).astype(BF16)
     zero = jnp.zeros((), BF16)
 
-    def window(sb, start):
+    def window(sb, start, slots):
+        width = min(SB, ncol - sb * SB)
         chunk = start // 128
         shift = start - chunk * 128
-        raw = edges_ref[pl.ds(pl.multiple_of(chunk * 8, 8), 8 * (KW // 128 + 1)), :]
-        raw = jnp.concatenate([raw[8 * i:8 * i + 8] for i in range(KW // 128 + 1)], axis=1)
-        rows = pltpu.roll(raw, KW + 128 - shift, 1)[:, :KW]
+        raw = edges_ref[pl.ds(pl.multiple_of(chunk * 8, 8), 8 * (slots // 128 + 1)), :]
+        raw = jnp.concatenate([raw[8 * i:8 * i + 8] for i in range(slots // 128 + 1)], axis=1)
+        rows = pltpu.roll(raw, slots + 128 - shift, 1)[:, :slots]
         dst = (rows[0:1] - dbase).astype(BF16)
         src = (rows[1:2] - F32(SB * sb)).astype(BF16)
-        hit = row_id == dst
+        tiled = lambda v: jnp.concatenate([v] * (slots // 128), axis=1)
+        hit = tiled(row_id) == dst
         d3 = jnp.concatenate([jnp.where(hit, part, zero) for part in bf16_parts(rows[2:3])], axis=0)
-        col_id = last_id if sb == nsb - 1 else iota_s
-        sel = jnp.where(col_id == src, jnp.ones((), BF16), zero)
+        col_id = hub_col.astype(BF16) if sb == nsb - 1 else iota_s
+        sel = jnp.where(tiled(col_id) == src, jnp.ones((), BF16), zero)
         out = lax.dot_general(d3, sel, (((1,), (1,)), ((), ())), preferred_element_type=F32)
-        return out[:DB] + (out[DB:2 * DB] + out[2 * DB:])
-
-    for sb in range(nsb):
-        a_ref[:, sb * SB:(sb + 1) * SB] = window(sb, starts_ref[0, db * nsb + sb])
+        return out[:DB] + (out[DB:2 * DB] + out[2 * DB:]), slice(sb * SB, sb * SB + width)
+
+    slots = [KW] * (nsb - 1) + [2 * KW]
+    over = None
     for sb in range(nsb):
         start = starts_ref[0, db * nsb + sb]
-        end = starts_ref[0, db * nsb + sb + 1]
-
-        def more(i, carry):
-            a_ref[:, sb * SB:(sb + 1) * SB] += window(sb, start + i * KW)
-            return carry
-
-        lax.fori_loop(1, (end - start + KW - 1) // KW, more, 0)
-
-
-def build_adjacency(starts, edges, hub_col, ndb, nsb):
+        more = starts_ref[0, db * nsb + sb + 1] - start - slots[sb]
+        over = more if over is None else jnp.maximum(over, more)
+        block, where = window(sb, start, slots[sb])
+        a_ref[:, where] = block
+
+    @pl.when(over > 0)
+    def _():
+        for sb in range(nsb):
+            start = starts_ref[0, db * nsb + sb] + slots[sb]
+            end = starts_ref[0, db * nsb + sb + 1]
+
+            def step(i, carry):
+                block, where = window(sb, start + i * KW, KW)
+                a_ref[:, where] += block
+                return carry
+
+            lax.fori_loop(0, (jnp.maximum(end - start, 0) + KW - 1) // KW, step, 0)
+
+
+def build_adjacency(starts, edges, hub_col, ndb, nsb, ncol):
     return pl.pallas_call(
-        functools.partial(build_kernel, ndb, nsb),
-        out_shape=jax.ShapeDtypeStruct((ndb * DB, nsb * SB), F32),
+        functools.partial(build_kernel, ndb, nsb, ncol),
+        out_shape=jax.ShapeDtypeStruct((ndb * DB, ncol), F32),
         grid_spec=pltpu.PrefetchScalarGridSpec(
             num_scalar_prefetch=1,
             grid=(ndb,),
             in_specs=[pl.BlockSpec(edges.shape, lambda i, s: (0, 0)), pl.BlockSpec(hub_col.shape, lambda i, s: (0, 0))],
-            out_specs=pl.BlockSpec((DB, nsb * SB), lambda i, s: (i, 0)),
+            out_specs=pl.BlockSpec((DB, ncol), lambda i, s: (i, 0)),
         ),
         name="build",
     )(starts, edges, hub_col)
@@ -156,9 +164,9 @@
         across(level, min(level - 1, 2), 0)
 
 
-def pre_kernel(dims, dst_ref, src_ref, valid_ref, w_ref, x_ref, w1_ref, w2_ref,
-               edges_ref, starts_ref, tab_ref, w2all_ref, inv_ref,
-               kref, wref, xin, w1in, w2in, tab, zout, xs, xr, w1s, w1r, w2s, w2r, zs, zr):
+def pre_kernel(dims, dst_ref, src_ref, valid_ref, w_ref, x_ref, w1_ref, hub_ref, send_ref, keep_ref,
+               edges_ref, starts_ref, tab_ref, inv_ref, hubcol_ref, myhub_ref, idx_ref,
+               kref, wref, xin, w1in, tab, zout, xs, xr, w1s, w1r, zs, zr):
     nfeat, ngraph, ndb, nsb = dims
     vert = x_ref.shape[0]
     part = vert // nfeat
@@ -180,13 +188,11 @@
     peers = range(1, nfeat)
     x_copies = [frdma(x_ref.at[quarter(fpeer(r))], xin.at[f], xs.at[r - 1], xr.at[r - 1], r) for r in peers]
     w1_copies = [frdma(w1_ref, w1in.at[f], w1s.at[r - 1], w1r.at[r - 1], r) for r in peers]
-    w2_copies = [frdma(w2_ref, w2in.at[f], w2s.at[r - 1], w2r.at[r - 1], r) for r in peers]
     z_copies = [frdma(zout.at[fpeer(r)], tab.at[quarter(f)], zs.at[r - 1], zr.at[r - 1], r) for r in peers]
     for copy in w1_copies + x_copies:
         copy.start()
     xin[f] = x_ref[quarter(f)]
     w1in[f] = w1_ref[...]
-    w2in[f] = w2_ref[...]
 
     dst, src = dst_ref[...], src_ref[...]
     key = (((dst // DB) * nsb + src // SB) << 15) | ((dst % DB) << 8) | (src % SB)
@@ -201,7 +207,33 @@
     wref[:used] = coef.reshape(used, 8, 128)
     kref[used:] = jnp.full((64 - used, 8, 128), nbucket << 15, F32)
     wref[used:] = jnp.zeros((64 - used, 8, 128), F32)
-    sort_levels(kref, wref, 1, 11)
+    sort_levels(kref, wref, 1, 12)
+
+    g, per = lax.axis_index("graph"), DB // ngraph
+    lane_id = lax.broadcasted_iota(jnp.int32, (DB, DB), 1).astype(F32)
+    row_id = lax.broadcasted_iota(jnp.int32, (DB, DB), 0).astype(F32)
+    down = lambda row: jnp.broadcast_to(row, (DB, DB)).T
+    ids = hub_ref[...].astype(F32)
+    owner = (hub_ref[...] // vert).astype(F32)
+    owner_down = down(owner)
+    earlier = (owner == owner_down) & (lane_id < row_id)
+    pos_down = owner_down * per + jnp.sum(jnp.where(earlier, F32(1), F32(0)), axis=1, keepdims=True)
+    pos = pos_down.T
+    base = (g * per).astype(F32)
+    first = (g * vert).astype(F32)
+    hubcol_ref[...] = jnp.broadcast_to(jnp.sum(jnp.where(pos == row_id, lane_id, F32(0)), axis=1, keepdims=True), (DB, DB))
+    lane_row = lax.broadcasted_iota(jnp.int32, (1, DB), 1)
+    target = (lane_row % per).astype(F32) + base
+    mine = jnp.sum(jnp.where(pos_down == target, down(ids), F32(0)), axis=0, keepdims=True) - first
+    myhub_ref[...] = jnp.where(lane_row < 3 * per, mine, F32(-1)).astype(jnp.int32)
+    mine_down = jnp.sum(jnp.where(pos == row_id + base, ids, F32(0)), axis=1, keepdims=True) - first
+    mine_down = jnp.broadcast_to(mine_down, (DB, DB))[:per].astype(jnp.int32)
+    rows = jnp.where(keep_ref[...] > 0, send_ref[...], -1).astype(F32)
+    nsend = rows.shape[1]
+    for p in range(ngraph):
+        for h in range(nsend // DB):
+            idx_ref[p, h * DB:(h + 1) * DB] = down(rows[p:p + 1, h * DB:(h + 1) * DB]).astype(jnp.int32)
+        idx_ref[p, nsend:] = mine_down
 
     for copy in w1_copies + x_copies:
         copy.wait_recv()
@@ -213,10 +245,10 @@
     z = z.astype(BF16)
     for q in range(nfeat):
         zout[q] = z[:, q * cols:(q + 1) * cols]
-    for copy in z_copies + w2_copies:
+    for copy in z_copies:
         copy.start()
     tab[quarter(f)] = zout[f]
-    sort_levels(kref, wref, 12, 16)
+    sort_levels(kref, wref, 13, 16)
 
     nb = starts_ref.shape[1]
     bound = (lax.broadcasted_iota(jnp.int32, (nb, 1), 0) << 15).astype(F32)
@@ -247,15 +279,14 @@
         for field, val in enumerate((edge_dst, edge_src, ww)):
             edges_ref[pl.ds(k * 8 + field, nl, stride=32), :] = val.T[:nl]
 
-    for copy in z_copies + w2_copies:
+    for copy in z_copies:
         copy.wait_recv()
     tab_ref[...] = tab[...]
-    w2all_ref[...] = w2in[...]
-    for copy in x_copies + w1_copies + w2_copies + z_copies:
+    for copy in x_copies + w1_copies + z_copies:
         copy.wait_send()
 
 
-def run_pre(nfeat, ngraph, ndb, nsb, dst, src, valid, w, x, w1, w2):
+def run_pre(nfeat, ngraph, ndb, nsb, dst, src, valid, w, x, w1, hubs, send, keep):
     vert, part = x.shape[0], x.shape[0] // nfeat
     cols = w1.shape[1] // nfeat
     nrows = dst.shape[0]
@@ -265,21 +296,22 @@
     shape = jax.ShapeDtypeStruct
     return pl.pallas_call(
         functools.partial(pre_kernel, (nfeat, ngraph, ndb, nsb)),
-        out_shape=[shape(((nrows + 4) * 8, 128), F32), shape((8, 384), jnp.int32), shape((vert, cols), BF16), shape((nfeat, *w2.shape), BF16), shape((1, cols), F32)],
-        in_specs=[vspec] * 7,
-        out_specs=[vspec] * 5,
+        out_shape=[shape(((nrows + 8) * 8, 128), F32), shape((8, 384), jnp.int32), shape((vert, cols), BF16), shape((1, cols), F32),
+                   shape((DB, DB), F32), shape((1, DB), jnp.int32), shape((ngraph, send.shape[1] + DB // ngraph, DB), jnp.int32)],
+        in_specs=[vspec] * 9,
+        out_specs=[vspec] * 7,
         scratch_shapes=[
-            vm((64, 8, 128), F32), vm((64, 8, 128), F32), vm((nfeat, part, x.shape[1]), BF16), vm((nfeat, *w1.shape), BF16), vm((nfeat, *w2.shape), BF16),
-            vm((vert, cols), BF16), vm((nfeat, part, cols), BF16), dma, dma, dma, dma, dma, dma, dma, dma,
+            vm((64, 8, 128), F32), vm((64, 8, 128), F32), vm((nfeat, part, x.shape[1]), BF16), vm((nfeat, *w1.shape), BF16),
+            vm((vert, cols), BF16), vm((nfeat, part, cols), BF16), dma, dma, dma, dma, dma, dma,
         ],
-        compiler_params=pltpu.CompilerParams(collective_id=0, has_side_effects=True, vmem_limit_bytes=40 * 2**20),
+        compiler_params=pltpu.CompilerParams(collective_id=0, has_side_effects=True, vmem_limit_bytes=62 * 2**20),
         name="pre",
-    )(dst, src, valid, w, x, w1, w2)
-
-
-def layers_kernel(dims, tabown_ref, w2in, idx_ref, myhub_ref, b1_ref, b2_ref, inv_ref, a_hbm, o_ref,
-                  a_v, acc, tot, tab1, tab2, zout, hsend, hin, halo, hubsend, hubrecv,
-                  a_sem, z2s, z2r, hs, hr, ps, pr, us, ur, ns, nr):
+    )(dst, src, valid, w, x, w1, hubs, send, keep)
+
+
+def layers_kernel(dims, tabown_ref, w2_ref, idx_ref, myhub_ref, b1_ref, inv_ref, a_hbm, o_ref,
+                  a_v, acc, tot, w2in, tab1, tab2, zout, hsend, hin, halo, hubsend, hubrecv,
+                  a_sem, w2s, w2r, z2s, z2r, hs, hr, ps, pr, us, ur, ns, nr):
     nfeat, ngraph, vert, nsend, per = dims
     part, rows_send = vert // nfeat, nsend + per
     nchunk = part // DB
@@ -309,10 +341,12 @@
         pl.semaphore_signal(barrier, inc=1, device_id={"graph": gpeer(r)}, device_id_type=MESH)
     pl.semaphore_wait(barrier, nfeat + ngraph - 2)
 
-    pad_rows = a_v.shape[1] - hub_base - ngraph * per
+    w2_copies = [frdma(w2_ref, w2in.at[f], w2s.at[r - 1], w2r.at[r - 1], r) for r in range(1, nfeat)]
+    for copy in w2_copies:
+        copy.start()
+    w2in[f] = w2_ref[...]
     for tab in (tab1, tab2):
         tab[pl.ds(pl.multiple_of(halo_base + g * nsend, nsend), nsend)] = jnp.zeros((nsend, tab.shape[1]), BF16)
-        tab[hub_base + ngraph * per:] = jnp.zeros((pad_rows, tab.shape[1]), BF16)
 
     cols = tab1.shape[1]
     tab1[:vert] = tabown_ref[...]
@@ -364,13 +398,21 @@
         return pltpu.make_async_copy(a_hbm.at[chunk(rb)], a_v.at[chunk(rb)], a_sem.at[rb])
 
     def own_part(tab, layer):
-        def one(rb, carry):
+        def one(rb):
+            acc[chunk(rb)] = product(a_v[chunk(rb), :vert], tab[:vert])
+
+        def four(i, carry):
             if layer == 0:
-                a_copy(rb).wait()
-            acc[chunk(rb)] = product(a_v[chunk(rb), :vert], tab[:vert])
+                for u in range(4):
+                    a_copy(4 * i + u).wait()
+            for u in range(4):
+                one(4 * i + u)
             return carry
 
-        lax.fori_loop(0, nblock + 1, one, 0)
+        lax.fori_loop(0, nblock // 4, four, 0)
+        if layer == 0:
+            a_copy(nblock).wait()
+        one(nblock)
 
     def far_part(tab, rb):
         return (acc[chunk(rb)] + product(a_v[chunk(rb), vert:], tab[vert:])) * inv
@@ -425,42 +467,34 @@
 
     bias1 = b1_ref[...]
 
-    def place(t):
-        i, rr = t // nfeat, lax.rem(t, nfeat)
-        q = fpeer(rr + 1)
-        return i, rr, q, q * nchunk + i
-
-    def rows1(t, carry):
-        @pl.when(t < nblock)
-        def _():
-            rb = place(t)[3]
+    def far1(i):
+        for r in range(1, nfeat + 1):
+            rb = fpeer(r) * nchunk + i
             acc[chunk(rb)] = far_part(tab1, rb)
 
-        @pl.when(t == LAG)
-        def _():
-            hub_totals(0)
-
-        @pl.when(t >= LAG)
-        def _():
-            i, rr, q, rb = place(t - LAG)
-            h = jnp.maximum(with_hubs(0, rb) + bias1, 0.0).astype(BF16)
-
-            @pl.when(rr < nfeat - 1)
-            def _():
+    def finish1(i):
+        for r in range(1, nfeat + 1):
+            q = fpeer(r)
+            h = jnp.maximum(with_hubs(0, q * nchunk + i) + bias1, 0.0).astype(BF16)
+            if r < nfeat:
                 hsend[q, chunk(i)] = h
-                h_copy(i, rr + 1).start()
-
-            @pl.when(rr == nfeat - 1)
-            def _():
+                h_copy(i, r).start()
+            else:
                 hin[f, chunk(i)] = h
 
-            @pl.when((rr == nfeat - 2) & (i > 0))
-            def _():
-                z2_chunk(i - 1)
-
+    far1(0)
+    hub_totals(0)
+    for copy in w2_copies:
+        copy.wait_recv()
+
+    def rows1(i, carry):
+        finish1(i - 1)
+        far1(i)
+        z2_chunk(i - 1)
         return carry
 
-    lax.fori_loop(0, nblock + LAG, rows1, 0)
+    lax.fori_loop(1, nchunk, rows1, 0)
+    finish1(nchunk - 1)
     z2_chunk(nchunk - 1)
     for i in range(nchunk):
         for r in range(1, nfeat):
@@ -470,25 +504,27 @@
     own_part(tab2, 1)
     wait_halo(tab2, 1)
     exchange_hubs(tab2, 1)
-    bias2 = b2_ref[...]
-
-    def rows2(t, carry):
-        @pl.when(t < nblock)
-        def _():
-            acc[chunk(t)] = far_part(tab2, t)
-
-        @pl.when(t == LAG)
-        def _():
-            hub_totals(1)
-
-        @pl.when(t >= LAG)
-        def _():
-            o_ref[chunk(t - LAG), :] = with_hubs(1, t - LAG) + bias2
-
+    def far2(i):
+        for u in range(4):
+            acc[chunk(4 * i + u)] = far_part(tab2, 4 * i + u)
+
+    def finish2(i):
+        for u in range(4):
+            o_ref[chunk(4 * i + u), :] = with_hubs(1, 4 * i + u)
+
+    far2(0)
+    hub_totals(1)
+
+    def rows2(i, carry):
+        far2(i)
+        finish2(i - 1)
         return carry
 
-    lax.fori_loop(0, nblock + LAG, rows2, 0)
-
+    lax.fori_loop(1, nblock // 4, rows2, 0)
+    finish2(nblock // 4 - 1)
+
+    for copy in w2_copies:
+        copy.wait_send()
     for i in range(nchunk):
         for r in range(1, nfeat):
             h_copy(i, r).wait_send()
@@ -500,7 +536,7 @@
             hub_copy(layer, r).wait_send()
 
 
-def run_layers(nfeat, ngraph, nsend, per, tab_own, w2, idx, myhub, b1, b2, inv, adj):
+def run_layers(nfeat, ngraph, nsend, per, tab_own, w2, idx, myhub, b1, inv, adj):
     vert = tab_own.shape[0]
     part, cols = vert // nfeat, b1.shape[1]
     nchunk, nblk = part // DB, adj.shape[0] // DB
@@ -511,18 +547,18 @@
     return pl.pallas_call(
         functools.partial(layers_kernel, (nfeat, ngraph, vert, nsend, per)),
         out_shape=jax.ShapeDtypeStruct((vert, cols), F32),
-        in_specs=[vspec] * 7 + [pl.BlockSpec(memory_space=pl.ANY)],
+        in_specs=[vspec] * 6 + [pl.BlockSpec(memory_space=pl.ANY)],
         out_specs=vspec,
         scratch_shapes=[
-            vm(adj.shape, F32), vm((adj.shape[0], cols), F32), vm((2, DB, cols), BF16),
+            vm(adj.shape, F32), vm((adj.shape[0], cols), F32), vm((2, DB, cols), BF16), vm((nfeat, *w2.shape), BF16),
             vm((adj.shape[1], cols), BF16), vm((adj.shape[1], cols), BF16), vm((nfeat, part, cols), BF16), vm((nfeat, part, cols), BF16),
             vm((nfeat, part, cols), BF16), vm((2, ngraph, nsend + per, cols), BF16), vm((2, ngraph * per, cols), F32), vm((2, ngraph, per, cols), F32),
-            dma(nblk), dma(nchunk, fr), dma(nchunk, fr),
+            dma(nblk), dma(fr), dma(fr), dma(nchunk, fr), dma(nchunk, fr),
             dma(2, gr), dma(2, gr), dma(2, gr), dma(2, gr), dma(2, gr), dma(2, gr), dma(nchunk, fr), dma(nchunk, fr),
         ],
         compiler_params=pltpu.CompilerParams(collective_id=1, has_side_effects=True, vmem_limit_bytes=62 * 2**20),
         name="layers",
-    )(tab_own, w2, idx, myhub, b1, b2, inv, adj)
+    )(tab_own, w2, idx, myhub, b1, inv, adj)
 
 
 def solution(mesh):
@@ -535,30 +571,14 @@
         nhub = hub_ids.shape[0]
         per = nhub // ngraph
         nsend = send_loc.shape[1]
-        me = lax.axis_index("graph")
         ndb = (vert + nhub) // DB
         table_rows = vert + ngraph * nsend + nhub
         nsb = -(-table_rows // SB)
-
-        owner = hub_ids // vert
-        ks = jnp.arange(nhub)
-        before = (owner[None, :] == owner[:, None]) & (ks[None, :] < ks[:, None])
-        pos = owner * per + jnp.sum(before.astype(jnp.int32), axis=1)
-        at_pos = pos[None, :] == ks[:, None]
-        hub_by_pos = jnp.sum(jnp.where(at_pos, hub_ids[None, :], 0), axis=1)
-        k_by_pos = jnp.sum(jnp.where(at_pos, ks[None, :], 0), axis=1)
-        my_hubs = lax.dynamic_slice(hub_by_pos, (me * per,), (per,)) - me * vert
-
         grid = lambda v: v.reshape(-1, 128)
-        edges, starts, tab_own, w2_all, inv = run_pre(nfeat, ngraph, ndb, nsb, grid(dst_loc), grid(src_loc), grid(valid_loc), grid(w_loc), x_loc, w_first, w_second)
-        hub_col = jnp.broadcast_to(k_by_pos.astype(F32)[:, None], (DB, 128))
-        adj = build_adjacency(starts, edges, hub_col, ndb, nsb)
-
-        idx = jnp.where(keep_loc > 0, send_loc, -1)
-        idx = jnp.concatenate([idx, jnp.broadcast_to(my_hubs[None, :], (ngraph, per))], axis=1)
-        idx = jnp.broadcast_to(idx[:, :, None], (*idx.shape, DB))
-        myhub = jnp.pad(jnp.concatenate([my_hubs] * 3), (0, DB - 3 * per), constant_values=-1)[None, :]
-        return run_layers(nfeat, ngraph, nsend, per, tab_own, w2_all, idx, myhub, b_first[None, :], b_second[None, :], inv, adj)
+        edges, starts, tab_own, inv, hub_col, myhub, idx = run_pre(
+            nfeat, ngraph, ndb, nsb, grid(dst_loc), grid(src_loc), grid(valid_loc), grid(w_loc), x_loc, w_first, hub_ids[None, :], send_loc, keep_loc)
+        adj = build_adjacency(starts, edges, hub_col, ndb, nsb, table_rows)
+        return run_layers(nfeat, ngraph, nsend, per, tab_own, w_second, idx, myhub, b_first[None, :], inv, adj) + b_second
 
     edge_spec = P(rows_axes)
     send_spec = P(rows_axes, None)

time: 152 us -> 133 us (0.88)
  Pallas kernels: 137 us -> 128 us
  local copies, waits for them, and re-layouts: 9.96 us -> 2.01 us
    pallas_call x1, Pallas kernels: 35.3 us -> 25.9 us  [build_adjacency(): pl.pallas_call(functools.partial(build_kernel, ndb, nsb, ncol), out_shape...]
    unnamed x24 -> x3, local copies, waits for them, and re-layouts: 7.38 us -> 2.01 us
    broadcast_in_dim x3 -> x0, local copies, waits for them, and re-layouts: 2.57 us -> none  [the longest x1 1.35 us: device_program(): idx = jnp.broadcast_to(idx[:, :, None], (*idx.shape, DB))]
    add x1, other arithmetic: 0.67 us -> 2.26 us  [device_program(): run_layers(nfeat, ngraph, nsend, per, tab_own, w_second, idx, myhub, b_fi...]
where the time goes in v3:
time: 133 us; the launch traced here: 132 us
  Pallas kernels  128 us (96%)
  other arithmetic  2.26 us (2%)
  local copies, waits for them, and re-layouts  2.01 us (2%)
    pallas_call x1, Pallas kernels, run_layers(): pl.pallas_call(functools.partial(layers_kernel, (nfeat, ngraph, vert, nse...  72.9 us
    pallas_call x1, Pallas kernels, run_pre(): pl.pallas_call(functools.partial(pre_kernel, (nfeat, ngraph, ndb, nsb)),...  29.1 us
    pallas_call x1, Pallas kernels, build_adjacency(): pl.pallas_call(functools.partial(build_kernel, ndb, nsb, ncol), out_shape...  25.9 us

profile of v3, /device:TPU:97, one launch (start us, length us, event | category | flops | bytes accessed | tf_op | source)
XLA Modules:
  0.0 132.2 jit_solution(15833823110335833977)
XLA Ops:
  0.0 2.0 %copy.13.x_ref = bf16[2048,75]{1,0:T(8,128)(2,1)} copy(bf16[2048,75]{0,1:T(8,128)(2,1)} %param.12) | data formatting | bytes 614400 | tf_op args[0]
  2.0 29.1 %pre.1 = (f32[2624,128]{1,0:T(8,128)}, s32[8,384]{1,0:T(8,128)}, bf16[2048,128]{1,0:T(8,128)(2,1)}, f32[1,128]{1,0:T(1,128)}, f32[128,128]{1,0:T(8,128)}, /*index=5*/s32[1,128]{1,0:T(1,128)}, s32[8,272,128]{2,1,0:T(8,128)}) custom-call(s32[320,128]{1,0:T(8,128)} %bitcast.6, s32[320,128]{1,0:T(8,128)} %bitcast.7, s32[320,128]{1,0:T(8,128)} %bitcast.8, ...), custom_call_target="tpu_custom_call" | custom-call | tf_op jit(solution)/shard_map/pre/pallas_call | solution.py:297
  31.1 25.9 %build.1.a_hbm = f32[2176,4224]{1,0:T(8,128)} custom-call(s32[8,384]{1,0:T(8,128)} %get-tuple-element.16.starts_ref, f32[2624,128]{1,0:T(8,128)} %get-tuple-element.17.edges_ref, f32[128,128]{1,0:T(8,128)} %get-tuple-element.18.hubcol_ref), custom_call_target="tpu_custom_call" | custom-call | tf_op jit(solution)/shard_map/build/pallas_call | solution.py:72
  57.0 0.0 copy-start
  57.0 72.9 %layers.1 = f32[2048,128]{1,0:T(8,128)} custom-call(bf16[2048,128]{1,0:T(8,128)(2,1)} %get-tuple-element.12.tabown_ref, bf16[128,512]{1,0:T(8,128)(2,1)} %w2_ref.1, s32[8,272,128]{2,1,0:T(8,128)} %get-tuple-element.13.idx_ref, s32[1,128]{1,0:T(1,128)} %get-tuple-element.14.myhub_ref, f32[1,128]{1,0:T(1,128)} %bitcast.11, ...), custom_call_target="tpu_custom_call" | custom-call | tf_op jit(solution)/shard_map/layers/pallas_call | solution.py:547
  129.9 0.0 copy-done
  129.9 2.3 %broadcast_add_fusion = f32[2048,128]{1,0:T(8,128)} fusion(f32[2048,128]{1,0:T(8,128)} %layers.1, f32[128]{0:T(128)S(1)} %copy-done), kind=kLoop, calls=%fused_computation | loop fusion | flops 262144 | bytes 2097664 | tf_op jit(solution)/shard_map/add | solution.py:581
Async XLA Ops:
  57.0 72.9 %copy-start = (f32[128]{0:T(128)S(1)}, f32[128]{0:T(128)}, u32[]{:S(2)}) copy-start(f32[128]{0:T(128)} %param.23) | copy-start | bytes 1540

commit v4 on v3

--- a/solution.py
+++ b/solution.py
@@ -78,6 +78,7 @@
             in_specs=[pl.BlockSpec(edges.shape, lambda i, s: (0, 0)), pl.BlockSpec(hub_col.shape, lambda i, s: (0, 0))],
             out_specs=pl.BlockSpec((DB, ncol), lambda i, s: (i, 0)),
         ),
+        compiler_params=pltpu.CompilerParams(vmem_limit_bytes=20 * 2**20),
         name="build",
     )(starts, edges, hub_col)
 
@@ -168,7 +169,7 @@
                edges_ref, starts_ref, tab_ref, inv_ref, hubcol_ref, myhub_ref, idx_ref,
                kref, wref, xin, w1in, tab, zout, xs, xr, w1s, w1r, zs, zr):
     nfeat, ngraph, ndb, nsb = dims
-    vert = x_ref.shape[0]
+    vert = x_ref.shape[1]
     part = vert // nfeat
     f = lax.axis_index("feat")
 
@@ -186,12 +187,12 @@
         pl.semaphore_signal(barrier, inc=1, device_id={"feat": fpeer(r)}, device_id_type=MESH)
     pl.semaphore_wait(barrier, nfeat - 1)
     peers = range(1, nfeat)
-    x_copies = [frdma(x_ref.at[quarter(fpeer(r))], xin.at[f], xs.at[r - 1], xr.at[r - 1], r) for r in peers]
+    x_copies = [frdma(x_ref.at[:, quarter(fpeer(r))], xin.at[f], xs.at[r - 1], xr.at[r - 1], r) for r in peers]
     w1_copies = [frdma(w1_ref, w1in.at[f], w1s.at[r - 1], w1r.at[r - 1], r) for r in peers]
     z_copies = [frdma(zout.at[fpeer(r)], tab.at[quarter(f)], zs.at[r - 1], zr.at[r - 1], r) for r in peers]
     for copy in w1_copies + x_copies:
         copy.start()
-    xin[f] = x_ref[quarter(f)]
+    xin[f] = x_ref[:, quarter(f)]
     w1in[f] = w1_ref[...]
 
     dst, src = dst_ref[...], src_ref[...]
@@ -207,7 +208,7 @@
     wref[:used] = coef.reshape(used, 8, 128)
     kref[used:] = jnp.full((64 - used, 8, 128), nbucket << 15, F32)
     wref[used:] = jnp.zeros((64 - used, 8, 128), F32)
-    sort_levels(kref, wref, 1, 12)
+    sort_levels(kref, wref, 1, 13)
 
     g, per = lax.axis_index("graph"), DB // ngraph
     lane_id = lax.broadcasted_iota(jnp.int32, (DB, DB), 1).astype(F32)
@@ -240,7 +241,7 @@
     cols = tab.shape[1]
     z = None
     for s in range(nfeat):
-        term = jnp.dot(xin[s], w1in[s], preferred_element_type=F32)
+        term = lax.dot_general(xin[s], w1in[s], (((0,), (0,)), ((), ())), preferred_element_type=F32)
         z = term if z is None else z + term
     z = z.astype(BF16)
     for q in range(nfeat):
@@ -248,7 +249,7 @@
     for copy in z_copies:
         copy.start()
     tab[quarter(f)] = zout[f]
-    sort_levels(kref, wref, 13, 16)
+    sort_levels(kref, wref, 14, 16)
 
     nb = starts_ref.shape[1]
     bound = (lax.broadcasted_iota(jnp.int32, (nb, 1), 0) << 15).astype(F32)
@@ -287,7 +288,7 @@
 
 
 def run_pre(nfeat, ngraph, ndb, nsb, dst, src, valid, w, x, w1, hubs, send, keep):
-    vert, part = x.shape[0], x.shape[0] // nfeat
+    vert, part = x.shape[1], x.shape[1] // nfeat
     cols = w1.shape[1] // nfeat
     nrows = dst.shape[0]
     vm = lambda shape, dt: pltpu.VMEM(shape, dt)
@@ -301,7 +302,7 @@
         in_specs=[vspec] * 9,
         out_specs=[vspec] * 7,
         scratch_shapes=[
-            vm((64, 8, 128), F32), vm((64, 8, 128), F32), vm((nfeat, part, x.shape[1]), BF16), vm((nfeat, *w1.shape), BF16),
+            vm((64, 8, 128), F32), vm((64, 8, 128), F32), vm((nfeat, x.shape[0], part), BF16), vm((nfeat, *w1.shape), BF16),
             vm((vert, cols), BF16), vm((nfeat, part, cols), BF16), dma, dma, dma, dma, dma, dma,
         ],
         compiler_params=pltpu.CompilerParams(collective_id=0, has_side_effects=True, vmem_limit_bytes=62 * 2**20),
@@ -331,7 +332,7 @@
     def grdma(src, dst, send, recv, r):
         return pltpu.make_async_remote_copy(src, dst, send, recv, device_id={"graph": gpeer(r)}, device_id_type=MESH)
 
-    for i in range(a_hbm.shape[0] // DB):
+    for i in [nblock] + [q * nchunk + c for c in range(nchunk) for q in range(nfeat)]:
         pltpu.make_async_copy(a_hbm.at[pl.ds(i * DB, DB)], a_v.at[pl.ds(i * DB, DB)], a_sem.at[i]).start()
 
     barrier = pltpu.get_barrier_semaphore()
@@ -397,22 +398,19 @@
     def a_copy(rb):
         return pltpu.make_async_copy(a_hbm.at[chunk(rb)], a_v.at[chunk(rb)], a_sem.at[rb])
 
-    def own_part(tab, layer):
-        def one(rb):
+    def own_blocks(tab, layer, blocks):
+        if layer == 0:
+            for rb in blocks:
+                a_copy(rb).wait()
+        for rb in blocks:
             acc[chunk(rb)] = product(a_v[chunk(rb), :vert], tab[:vert])
 
-        def four(i, carry):
-            if layer == 0:
-                for u in range(4):
-                    a_copy(4 * i + u).wait()
-            for u in range(4):
-                one(4 * i + u)
+    def own_chunks(tab, layer, count):
+        def one(i, carry):
+            own_blocks(tab, layer, [q * nchunk + i for q in range(nfeat)])
             return carry
 
-        lax.fori_loop(0, nblock // 4, four, 0)
-        if layer == 0:
-            a_copy(nblock).wait()
-        one(nblock)
+        lax.fori_loop(0, count, one, 0)
 
     def far_part(tab, rb):
         return (acc[chunk(rb)] + product(a_v[chunk(rb), vert:], tab[vert:])) * inv
@@ -442,7 +440,8 @@
         return acc[chunk(rb)] + jnp.dot(sel, tot[layer], preferred_element_type=F32)
 
     start_halo(tab1, 0)
-    own_part(tab1, 0)
+    own_blocks(tab1, 0, [nblock])
+    own_chunks(tab1, 0, nchunk - 1)
     wait_halo(tab1, 0)
     exchange_hubs(tab1, 0)
     def h_copy(i, r):
@@ -487,21 +486,27 @@
     for copy in w2_copies:
         copy.wait_recv()
 
+    finish1(0)
+    own_blocks(tab1, 0, [q * nchunk + nchunk - 1 for q in range(nfeat)])
+    far1(1)
+
     def rows1(i, carry):
         finish1(i - 1)
+        z2_chunk(i - 2)
         far1(i)
-        z2_chunk(i - 1)
         return carry
 
-    lax.fori_loop(1, nchunk, rows1, 0)
+    lax.fori_loop(2, nchunk, rows1, 0)
     finish1(nchunk - 1)
+    z2_chunk(nchunk - 2)
     z2_chunk(nchunk - 1)
     for i in range(nchunk):
         for r in range(1, nfeat):
             z2_copy(i, r).wait_recv()
 
     start_halo(tab2, 1)
-    own_part(tab2, 1)
+    own_blocks(tab2, 1, [nblock])
+    own_chunks(tab2, 1, nchunk)
     wait_halo(tab2, 1)
     exchange_hubs(tab2, 1)
     def far2(i):
@@ -512,16 +517,17 @@
         for u in range(4):
             o_ref[chunk(4 * i + u), :] = with_hubs(1, 4 * i + u)
 
-    far2(0)
+    lag = nblock // 4 - 1
+
+    def far2_only(i, carry):
+        far2(i)
+        return carry
+
+    lax.fori_loop(0, lag, far2_only, 0)
     hub_totals(1)
-
-    def rows2(i, carry):
-        far2(i)
-        finish2(i - 1)
-        return carry
-
-    lax.fori_loop(1, nblock // 4, rows2, 0)
-    finish2(nblock // 4 - 1)
+    far2(lag)
+    for i in range(lag + 1):
+        finish2(i)
 
     for copy in w2_copies:
         copy.wait_send()
@@ -556,7 +562,7 @@
             dma(nblk), dma(fr), dma(fr), dma(nchunk, fr), dma(nchunk, fr),
             dma(2, gr), dma(2, gr), dma(2, gr), dma(2, gr), dma(2, gr), dma(2, gr), dma(nchunk, fr), dma(nchunk, fr),
         ],
-        compiler_params=pltpu.CompilerParams(collective_id=1, has_side_effects=True, vmem_limit_bytes=62 * 2**20),
+        compiler_params=pltpu.CompilerParams(collective_id=1, has_side_effects=True, vmem_limit_bytes=52 * 2**20),
         name="layers",
     )(tab_own, w2, idx, myhub, b1, inv, adj)
 
@@ -576,7 +582,7 @@
         nsb = -(-table_rows // SB)
         grid = lambda v: v.reshape(-1, 128)
         edges, starts, tab_own, inv, hub_col, myhub, idx = run_pre(
-            nfeat, ngraph, ndb, nsb, grid(dst_loc), grid(src_loc), grid(valid_loc), grid(w_loc), x_loc, w_first, hub_ids[None, :], send_loc, keep_loc)
+            nfeat, ngraph, ndb, nsb, grid(dst_loc), grid(src_loc), grid(valid_loc), grid(w_loc), x_loc.T, w_first, hub_ids[None, :], send_loc, keep_loc)
         adj = build_adjacency(starts, edges, hub_col, ndb, nsb, table_rows)
         return run_layers(nfeat, ngraph, nsend, per, tab_own, w_second, idx, myhub, b_first[None, :], inv, adj) + b_second
 

time: 133 us -> 115 us (0.86)
  Pallas kernels: 128 us -> 111 us
    pallas_call x1, Pallas kernels: 72.9 us -> 61.3 us  [run_layers(): pl.pallas_call(functools.partial(layers_kernel, (nfeat, ngraph, vert, nse...]
    pallas_call x1, Pallas kernels: 29.1 us -> 25.3 us  [run_pre(): pl.pallas_call(functools.partial(pre_kernel, (nfeat, ngraph, ndb, nsb)),...]
    pallas_call x1, Pallas kernels: 25.9 us -> 24.5 us  [build_adjacency(): pl.pallas_call(functools.partial(build_kernel, ndb, nsb, ncol), out_shape...]
    unnamed x3 -> x18, local copies, waits for them, and re-layouts: 2.01 us -> 2.89 us
where the time goes in v4:
time: 115 us
  Pallas kernels  111 us (97%)
  local copies, waits for them, and re-layouts  2.89 us (3%)
    pallas_call x1, Pallas kernels, run_layers(): pl.pallas_call(functools.partial(layers_kernel, (nfeat, ngraph, vert, nse...  61.3 us
    pallas_call x1, Pallas kernels, run_pre(): pl.pallas_call(functools.partial(pre_kernel, (nfeat, ngraph, ndb, nsb)),...  25.3 us
    pallas_call x1, Pallas kernels, build_adjacency(): pl.pallas_call(functools.partial(build_kernel, ndb, nsb, ncol), out_shape...  24.5 us
    unnamed x18, local copies, waits for them, and re-layouts  2.89 us

profile of v4, /device:TPU:97, one launch (start us, length us, event | category | flops | bytes accessed | tf_op | source)
XLA Modules:
  0.0 115.1 jit_solution(8648992026771361961)
XLA Ops:
  0.0 25.3 %pre.1 = (f32[2624,128]{1,0:T(8,128)}, s32[8,384]{1,0:T(8,128)}, bf16[2048,128]{1,0:T(8,128)(2,1)}, f32[1,128]{1,0:T(1,128)}, f32[128,128]{1,0:T(8,128)}, /*index=5*/s32[1,128]{1,0:T(1,128)}, s32[8,272,128]{2,1,0:T(8,128)}) custom-call(s32[320,128]{1,0:T(8,128)} %bitcast.9, s32[320,128]{1,0:T(8,128)} %bitcast.10, s32[320,128]{1,0:T(8,128)} %bitcast.11, ...), custom_call_target="tpu_custom_call" | custom-call | tf_op jit(solution)/shard_map/pre/pallas_call | solution.py:298
  25.3 0.0 copy-start
  25.3 1.3 %copy-done = f32[2624,128]{1,0:T(8,128)S(1)} copy-done((f32[2624,128]{1,0:T(8,128)S(1)}, f32[2624,128]{1,0:T(8,128)}, u32[]{:S(2)}) %copy-start) | copy-done | bytes 1343512
  26.6 0.0 copy-start.3
  26.6 0.8 copy-done.3
  27.5 0.0 copy-start.4
  27.5 0.7 copy-done.4
  28.2 0.0 copy-start.1
  28.2 0.0 copy-start.2
  28.2 0.0 copy-start.5
  28.2 0.0 copy-start.6
  28.2 0.0 copy-start.7
  28.2 24.5 %build.1.a_hbm = f32[2176,4224]{1,0:T(8,128)} custom-call(s32[8,384]{1,0:T(8,128)S(1)} %copy-done.4, f32[2624,128]{1,0:T(8,128)S(1)} %copy-done, f32[128,128]{1,0:T(8,128)S(1)} %copy-done.3), custom_call_target="tpu_custom_call" | custom-call | tf_op jit(solution)/shard_map/build/pallas_call | solution.py:72
  52.7 0.0 copy-done.1
  52.7 0.0 copy-done.2
  52.7 0.0 copy-done.5
  52.7 0.0 copy-done.6
  52.7 0.0 copy-done.7
  52.7 0.0 copy-start.8
  52.7 61.3 %layers.1 = f32[2048,128]{1,0:T(8,128)S(1)} custom-call(bf16[2048,128]{1,0:T(8,128)(2,1)S(1)} %copy-done.1, bf16[128,512]{1,0:T(8,128)(2,1)S(1)} %copy-done.2, s32[8,272,128]{2,1,0:T(8,128)} %get-tuple-element.13.idx_ref, s32[1,128]{1,0:T(1,128)S(1)} %copy-done.7, f32[1,128]{1,0:T(1,128)S(1)} %bitcast.7, f32[1,128]{1,0:T(1,128)S(1)} %copy-done.6, ...), custom_call_target="tpu_custom_call" | custom-call | tf_op jit(solution)/shard_map/layers/pallas_call | solution.py:553
  114.0 0.0 copy-done.8
  114.0 1.0 broadcast_add_fusion
Async XLA Ops:
  25.3 1.3 %copy-start = (f32[2624,128]{1,0:T(8,128)S(1)}, f32[2624,128]{1,0:T(8,128)}, u32[]{:S(2)}) copy-start(f32[2624,128]{1,0:T(8,128)} %get-tuple-element.17.edges_ref) | copy-start | bytes 4030468
  26.6 0.8 copy-start.3
  27.5 0.7 copy-start.4
  28.2 24.5 %copy-start.1 = (bf16[2048,128]{1,0:T(8,128)(2,1)S(1)}, bf16[2048,128]{1,0:T(8,128)(2,1)}, u32[]{:S(2)}) copy-start(bf16[2048,128]{1,0:T(8,128)(2,1)} %get-tuple-element.12.tabown_ref) | copy-start | bytes 1572868
  28.2 24.5 %copy-start.2 = (bf16[128,512]{1,0:T(8,128)(2,1)S(1)}, bf16[128,512]{1,0:T(8,128)(2,1)}, u32[]{:S(2)}) copy-start(bf16[128,512]{1,0:T(8,128)(2,1)} %w2_ref.1) | copy-start | bytes 393220
  28.2 24.5 %copy-start.5 = (f32[128]{0:T(128)S(1)}, f32[128]{0:T(128)}, u32[]{:S(2)}) copy-start(f32[128]{0:T(128)} %param.22) | copy-start | bytes 1540
  28.2 24.5 %copy-start.6 = (f32[1,128]{1,0:T(1,128)S(1)}, f32[1,128]{1,0:T(1,128)}, u32[]{:S(2)}) copy-start(f32[1,128]{1,0:T(1,128)} %get-tuple-element.15.inv_ref) | copy-start | bytes 1540
  28.2 24.5 %copy-start.7 = (s32[1,128]{1,0:T(1,128)S(1)}, s32[1,128]{1,0:T(1,128)}, u32[]{:S(2)}) copy-start(s32[1,128]{1,0:T(1,128)} %get-tuple-element.14.myhub_ref) | copy-start | bytes 1540
  52.7 61.3 %copy-start.8 = (f32[128]{0:T(128)S(1)}, f32[128]{0:T(128)}, u32[]{:S(2)}) copy-start(f32[128]{0:T(128)} %param.23) | copy-start | bytes 1540

commit v5 on v4

--- a/solution.py
+++ b/solution.py
@@ -78,7 +78,7 @@
             in_specs=[pl.BlockSpec(edges.shape, lambda i, s: (0, 0)), pl.BlockSpec(hub_col.shape, lambda i, s: (0, 0))],
             out_specs=pl.BlockSpec((DB, ncol), lambda i, s: (i, 0)),
         ),
-        compiler_params=pltpu.CompilerParams(vmem_limit_bytes=20 * 2**20),
+        compiler_params=pltpu.CompilerParams(vmem_limit_bytes=62 * 2**20),
         name="build",
     )(starts, edges, hub_col)
 
@@ -166,7 +166,7 @@
 
 
 def pre_kernel(dims, dst_ref, src_ref, valid_ref, w_ref, x_ref, w1_ref, hub_ref, send_ref, keep_ref,
-               edges_ref, starts_ref, tab_ref, inv_ref, hubcol_ref, myhub_ref, idx_ref,
+               edges_ref, starts_ref, tab_ref, inv_ref, hubcol_ref, myhub_ref, high_ref, low_ref,
                kref, wref, xin, w1in, tab, zout, xs, xr, w1s, w1r, zs, zr):
     nfeat, ngraph, ndb, nsb = dims
     vert = x_ref.shape[1]
@@ -185,16 +185,6 @@
     barrier = pltpu.get_barrier_semaphore()
     for r in range(1, nfeat):
         pl.semaphore_signal(barrier, inc=1, device_id={"feat": fpeer(r)}, device_id_type=MESH)
-    pl.semaphore_wait(barrier, nfeat - 1)
-    peers = range(1, nfeat)
-    x_copies = [frdma(x_ref.at[:, quarter(fpeer(r))], xin.at[f], xs.at[r - 1], xr.at[r - 1], r) for r in peers]
-    w1_copies = [frdma(w1_ref, w1in.at[f], w1s.at[r - 1], w1r.at[r - 1], r) for r in peers]
-    z_copies = [frdma(zout.at[fpeer(r)], tab.at[quarter(f)], zs.at[r - 1], zr.at[r - 1], r) for r in peers]
-    for copy in w1_copies + x_copies:
-        copy.start()
-    xin[f] = x_ref[:, quarter(f)]
-    w1in[f] = w1_ref[...]
-
     dst, src = dst_ref[...], src_ref[...]
     key = (((dst // DB) * nsb + src // SB) << 15) | ((dst % DB) << 8) | (src % SB)
     nbucket = ndb * nsb
@@ -208,6 +198,16 @@
     wref[:used] = coef.reshape(used, 8, 128)
     kref[used:] = jnp.full((64 - used, 8, 128), nbucket << 15, F32)
     wref[used:] = jnp.zeros((64 - used, 8, 128), F32)
+    pl.semaphore_wait(barrier, nfeat - 1)
+    peers = range(1, nfeat)
+    x_copies = [frdma(x_ref.at[:, quarter(fpeer(r))], xin.at[f], xs.at[r - 1], xr.at[r - 1], r) for r in peers]
+    w1_copies = [frdma(w1_ref, w1in.at[f], w1s.at[r - 1], w1r.at[r - 1], r) for r in peers]
+    z_copies = [frdma(zout.at[fpeer(r)], tab.at[quarter(f)], zs.at[r - 1], zr.at[r - 1], r) for r in peers]
+    for copy in w1_copies + x_copies:
+        copy.start()
+    xin[f] = x_ref[:, quarter(f)]
+    w1in[f] = w1_ref[...]
+
     sort_levels(kref, wref, 1, 13)
 
     g, per = lax.axis_index("graph"), DB // ngraph
@@ -228,13 +228,19 @@
     mine = jnp.sum(jnp.where(pos_down == target, down(ids), F32(0)), axis=0, keepdims=True) - first
     myhub_ref[...] = jnp.where(lane_row < 3 * per, mine, F32(-1)).astype(jnp.int32)
     mine_down = jnp.sum(jnp.where(pos == row_id + base, ids, F32(0)), axis=1, keepdims=True) - first
-    mine_down = jnp.broadcast_to(mine_down, (DB, DB))[:per].astype(jnp.int32)
+    mine_down = jnp.broadcast_to(mine_down, (DB, DB))[:per]
     rows = jnp.where(keep_ref[...] > 0, send_ref[...], -1).astype(F32)
     nsend = rows.shape[1]
+
+    def put_index(p, where, val):
+        high = jnp.floor(val * F32(1.0 / DB))
+        high_ref[p, where] = high.astype(BF16)
+        low_ref[p, where] = (val - high * DB).astype(BF16)
+
     for p in range(ngraph):
         for h in range(nsend // DB):
-            idx_ref[p, h * DB:(h + 1) * DB] = down(rows[p:p + 1, h * DB:(h + 1) * DB]).astype(jnp.int32)
-        idx_ref[p, nsend:] = mine_down
+            put_index(p, slice(h * DB, (h + 1) * DB), down(rows[p:p + 1, h * DB:(h + 1) * DB]))
+        put_index(p, slice(nsend, nsend + per), mine_down)
 
     for copy in w1_copies + x_copies:
         copy.wait_recv()
@@ -298,9 +304,9 @@
     return pl.pallas_call(
         functools.partial(pre_kernel, (nfeat, ngraph, ndb, nsb)),
         out_shape=[shape(((nrows + 8) * 8, 128), F32), shape((8, 384), jnp.int32), shape((vert, cols), BF16), shape((1, cols), F32),
-                   shape((DB, DB), F32), shape((1, DB), jnp.int32), shape((ngraph, send.shape[1] + DB // ngraph, DB), jnp.int32)],
+                   shape((DB, DB), F32), shape((1, DB), jnp.int32), *[shape((ngraph, send.shape[1] + DB // ngraph, DB), BF16)] * 2],
         in_specs=[vspec] * 9,
-        out_specs=[vspec] * 7,
+        out_specs=[vspec] * 8,
         scratch_shapes=[
             vm((64, 8, 128), F32), vm((64, 8, 128), F32), vm((nfeat, x.shape[0], part), BF16), vm((nfeat, *w1.shape), BF16),
             vm((vert, cols), BF16), vm((nfeat, part, cols), BF16), dma, dma, dma, dma, dma, dma,
@@ -310,7 +316,7 @@
     )(dst, src, valid, w, x, w1, hubs, send, keep)
 
 
-def layers_kernel(dims, tabown_ref, w2_ref, idx_ref, myhub_ref, b1_ref, inv_ref, a_hbm, o_ref,
+def layers_kernel(dims, tabown_ref, w2_ref, high_ref, low_ref, myhub_ref, b1_ref, inv_ref, a_hbm, o_ref,
                   a_v, acc, tot, w2in, tab1, tab2, zout, hsend, hin, halo, hubsend, hubrecv,
                   a_sem, w2s, w2r, z2s, z2r, hs, hr, ps, pr, us, ur, ns, nr):
     nfeat, ngraph, vert, nsend, per = dims
@@ -352,10 +358,12 @@
     cols = tab1.shape[1]
     tab1[:vert] = tabown_ref[...]
 
-    lane = lax.broadcasted_iota(jnp.int32, (1, DB), 1)
-
-    def select_rows(tab, idx):
-        pieces = [jnp.where(idx == lane + DB * j, F32(1), F32(0)).astype(BF16) for j in range(vert // DB)]
+    lane = lax.broadcasted_iota(jnp.int32, (1, DB), 1).astype(F32).astype(BF16)
+
+    def select_rows(tab, high, low):
+        zero = jnp.zeros((), BF16)
+        hot = jnp.where(low == lane, jnp.ones((), BF16), zero)
+        pieces = [jnp.where(high == jnp.full((), j, BF16), hot, zero) for j in range(vert // DB)]
         return jnp.dot(jnp.concatenate(pieces, axis=1), tab[:vert], preferred_element_type=F32).astype(BF16)
 
     def halo_copies(tab, layer, r):
@@ -370,13 +378,13 @@
     def start_halo(tab, layer):
         def one(r, carry):
             p = gpeer(r)
-            halo[layer, p] = select_rows(tab, idx_ref[p])
+            halo[layer, p] = select_rows(tab, high_ref[p], low_ref[p])
             for copy in halo_copies(tab, layer, r):
                 copy.start()
             return carry
 
         lax.fori_loop(1, ngraph, one, 0)
-        tab[pl.ds(pl.multiple_of(hub_base + g * per, per), per)] = select_rows(tab, idx_ref[g, nsend:])
+        tab[pl.ds(pl.multiple_of(hub_base + g * per, per), per)] = select_rows(tab, high_ref[g, nsend:], low_ref[g, nsend:])
 
     def wait_halo(tab, layer):
         def arrive(r, carry):
@@ -499,14 +507,40 @@
     lax.fori_loop(2, nchunk, rows1, 0)
     finish1(nchunk - 1)
     z2_chunk(nchunk - 2)
+
+    def wait_z2(chunks):
+        for i in chunks:
+            for r in range(1, nfeat):
+                z2_copy(i, r).wait_recv()
+
+    half = nchunk // 2
+
+    def own_half(rb, c):
+        start = [q * part + c * DB for q in range(nfeat)]
+        a = jnp.concatenate([a_v[chunk(rb), s:s + half * DB] for s in start], axis=1)
+        return product(a, jnp.concatenate([tab2[s:s + half * DB] for s in start], axis=0))
+
+    def first_half(i, carry):
+        for u in range(4):
+            acc[chunk(4 * i + u)] = own_half(4 * i + u, 0)
+        return carry
+
+    wait_z2(range(half))
+    lax.fori_loop(0, nblock // 8, first_half, 0)
     z2_chunk(nchunk - 1)
-    for i in range(nchunk):
-        for r in range(1, nfeat):
-            z2_copy(i, r).wait_recv()
+    lax.fori_loop(nblock // 8, nblock // 4, first_half, 0)
+    acc[chunk(nblock)] = own_half(nblock, 0)
+    wait_z2(range(half, nchunk))
 
     start_halo(tab2, 1)
-    own_blocks(tab2, 1, [nblock])
-    own_chunks(tab2, 1, nchunk)
+
+    def second_half(i, carry):
+        for u in range(4):
+            acc[chunk(4 * i + u)] += own_half(4 * i + u, half)
+        return carry
+
+    acc[chunk(nblock)] += own_half(nblock, half)
+    lax.fori_loop(0, nblock // 4, second_half, 0)
     wait_halo(tab2, 1)
     exchange_hubs(tab2, 1)
     def far2(i):
@@ -542,7 +576,7 @@
             hub_copy(layer, r).wait_send()
 
 
-def run_layers(nfeat, ngraph, nsend, per, tab_own, w2, idx, myhub, b1, inv, adj):
+def run_layers(nfeat, ngraph, nsend, per, tab_own, w2, high, low, myhub, b1, inv, adj):
     vert = tab_own.shape[0]
     part, cols = vert // nfeat, b1.shape[1]
     nchunk, nblk = part // DB, adj.shape[0] // DB
@@ -553,7 +587,7 @@
     return pl.pallas_call(
         functools.partial(layers_kernel, (nfeat, ngraph, vert, nsend, per)),
         out_shape=jax.ShapeDtypeStruct((vert, cols), F32),
-        in_specs=[vspec] * 6 + [pl.BlockSpec(memory_space=pl.ANY)],
+        in_specs=[vspec] * 7 + [pl.BlockSpec(memory_space=pl.ANY)],
         out_specs=vspec,
         scratch_shapes=[
             vm(adj.shape, F32), vm((adj.shape[0], cols), F32), vm((2, DB, cols), BF16), vm((nfeat, *w2.shape), BF16),
@@ -564,7 +598,7 @@
         ],
         compiler_params=pltpu.CompilerParams(collective_id=1, has_side_effects=True, vmem_limit_bytes=52 * 2**20),
         name="layers",
-    )(tab_own, w2, idx, myhub, b1, inv, adj)
+    )(tab_own, w2, high, low, myhub, b1, inv, adj)
 
 
 def solution(mesh):
@@ -581,10 +615,10 @@
         table_rows = vert + ngraph * nsend + nhub
         nsb = -(-table_rows // SB)
         grid = lambda v: v.reshape(-1, 128)
-        edges, starts, tab_own, inv, hub_col, myhub, idx = run_pre(
+        edges, starts, tab_own, inv, hub_col, myhub, high, low = run_pre(
             nfeat, ngraph, ndb, nsb, grid(dst_loc), grid(src_loc), grid(valid_loc), grid(w_loc), x_loc.T, w_first, hub_ids[None, :], send_loc, keep_loc)
         adj = build_adjacency(starts, edges, hub_col, ndb, nsb, table_rows)
-        return run_layers(nfeat, ngraph, nsend, per, tab_own, w_second, idx, myhub, b_first[None, :], inv, adj) + b_second
+        return run_layers(nfeat, ngraph, nsend, per, tab_own, w_second, high, low, myhub, b_first[None, :], inv, adj) + b_second
 
     edge_spec = P(rows_axes)
     send_spec = P(rows_axes, None)

time: 115 us -> 114 us (level)
  local copies, waits for them, and re-layouts: 2.89 us -> 0.03 us
  other arithmetic: 1.04 us -> 2.26 us
    unnamed x18 -> x16, local copies, waits for them, and re-layouts: 2.89 us -> 0.03 us
    pallas_call x1, Pallas kernels: 24.5 us -> 26 us  [build_adjacency(): pl.pallas_call(functools.partial(build_kernel, ndb, nsb, ncol), out_shape...]
    add x1, other arithmetic: 1.04 us -> 2.26 us  [device_program(): run_layers(nfeat, ngraph, nsend, per, tab_own, w_second, high, low, myhub...]
where the time goes in v5:
time: 114 us
  Pallas kernels  112 us (98%)
  other arithmetic  2.26 us (2%)
    pallas_call x1, Pallas kernels, run_layers(): pl.pallas_call(functools.partial(layers_kernel, (nfeat, ngraph, vert, nse...  60.7 us
    pallas_call x1, Pallas kernels, build_adjacency(): pl.pallas_call(functools.partial(build_kernel, ndb, nsb, ncol), out_shape...  26 us
    pallas_call x1, Pallas kernels, run_pre(): pl.pallas_call(functools.partial(pre_kernel, (nfeat, ngraph, ndb, nsb)),...  25.1 us

profile of v5, /device:TPU:97, one launch (start us, length us, event | category | flops | bytes accessed | tf_op | source)
XLA Modules:
  0.0 114.2 jit_solution(4675452639683494459)
XLA Ops:
  0.0 0.0 copy-start.4
  0.0 0.0 copy-start.3
  0.0 25.1 %pre.1 = (f32[2624,128]{1,0:T(8,128)}, s32[8,384]{1,0:T(8,128)}, bf16[2048,128]{1,0:T(8,128)(2,1)}, f32[1,128]{1,0:T(1,128)}, f32[128,128]{1,0:T(8,128)}, /*inde...) custom-call(s32[320,128]{1,0:T(8,128)} %bitcast.9, s32[320,128]{1,0:T(8,128)} %bitcast.10, ...), custom_call_target="tpu_custom_call" | custom-call | tf_op jit(solution)/shard_map/pre/pallas_call | solution.py:304
  25.1 0.0 copy-start
  25.1 0.0 copy-start.1
  25.1 0.0 copy-start.2
  25.1 0.0 copy-start.5
  25.1 0.0 copy-start.6
  25.1 0.0 copy-start.7
  25.1 26.0 %build.1.a_hbm = f32[2176,4224]{1,0:T(8,128)} custom-call(s32[8,384]{1,0:T(8,128)} %get-tuple-element.18.starts_ref, f32[2624,128]{1,0:T(8,128)} %get-tuple-element.19.edges_ref, f32[128,128]{1,0:T(8,128)} %get-tuple-element.20.hubcol_ref), custom_call_target="tpu_custom_call" | custom-call | tf_op jit(solution)/shard_map/build/pallas_call | solution.py:72
  51.1 0.0 copy-done.4
  51.1 0.0 copy-done.3
  51.2 0.0 copy-done
  51.2 0.0 copy-done.1
  51.2 0.0 copy-done.2
  51.2 0.0 copy-done.5
  51.2 0.0 copy-done.6
  51.2 60.7 %layers.1 = f32[2048,128]{1,0:T(8,128)} custom-call(bf16[2048,128]{1,0:T(8,128)(2,1)S(1)} %copy-done.2, bf16[128,512]{1,0:T(8,128)(2,1)S(1)} %copy-done.3, bf16[8,272,128]{2,1,0:T(8,128)(2,1)S(1)} %copy-done, bf16[8,272,128]{2,1,0:T(8,128)(2,1)S(1)} %copy-done.1, s32[1,128]{1,0:T(1,128)S(1)} %copy-done.6, f32[1,128]{1,0:T(1,128)S(1)} %bitcast.7, ...), custom_call_target="tpu_custom_call" | custom-call | tf_op jit(solution)/shard_map/layers/pallas_call | solution.py:587
  111.9 0.0 copy-done.7
  112.0 2.3 %broadcast_add_fusion = f32[2048,128]{1,0:T(8,128)} fusion(f32[2048,128]{1,0:T(8,128)} %layers.1, f32[128]{0:T(128)S(1)} %copy-done.7), kind=kLoop, calls=%fused_computation | loop fusion | flops 262144 | bytes 2097664 | tf_op jit(solution)/shard_map/add | solution.py:621
Async XLA Ops:
  0.0 51.1 %copy-start.4 = (f32[128]{0:T(128)S(1)}, f32[128]{0:T(128)}, u32[]{:S(2)}) copy-start(f32[128]{0:T(128)} %param.22) | copy-start | bytes 1540
  0.0 51.1 %copy-start.3 = (bf16[128,512]{1,0:T(8,128)(2,1)S(1)}, bf16[128,512]{1,0:T(8,128)(2,1)}, u32[]{:S(2)}) copy-start(bf16[128,512]{1,0:T(8,128)(2,1)} %w2_ref.1) | copy-start | bytes 393220
  25.1 26.1 %copy-start = (bf16[8,272,128]{2,1,0:T(8,128)(2,1)S(1)}, bf16[8,272,128]{2,1,0:T(8,128)(2,1)}, u32[]{:S(2)}) copy-start(bf16[8,272,128]{2,1,0:T(8,128)(2,1)} %get-tuple-element.14.high_ref) | copy-start | bytes 1671172
  25.1 26.1 %copy-start.1 = (bf16[8,272,128]{2,1,0:T(8,128)(2,1)S(1)}, bf16[8,272,128]{2,1,0:T(8,128)(2,1)}, u32[]{:S(2)}) copy-start(bf16[8,272,128]{2,1,0:T(8,128)(2,1)} %get-tuple-element.15.low_ref) | copy-start | bytes 1671172
  25.1 26.1 %copy-start.2 = (bf16[2048,128]{1,0:T(8,128)(2,1)S(1)}, bf16[2048,128]{1,0:T(8,128)(2,1)}, u32[]{:S(2)}) copy-start(bf16[2048,128]{1,0:T(8,128)(2,1)} %get-tuple-element.13.tabown_ref) | copy-start | bytes 1572868
  25.1 26.1 %copy-start.5 = (f32[1,128]{1,0:T(1,128)S(1)}, f32[1,128]{1,0:T(1,128)}, u32[]{:S(2)}) copy-start(f32[1,128]{1,0:T(1,128)} %get-tuple-element.17.inv_ref) | copy-start | bytes 1540
  25.1 26.1 %copy-start.6 = (s32[1,128]{1,0:T(1,128)S(1)}, s32[1,128]{1,0:T(1,128)}, u32[]{:S(2)}) copy-start(s32[1,128]{1,0:T(1,128)} %get-tuple-element.16.myhub_ref) | copy-start | bytes 1540
  25.1 86.8 %copy-start.7 = (f32[128]{0:T(128)S(1)}, f32[128]{0:T(128)}, u32[]{:S(2)}) copy-start(f32[128]{0:T(128)} %param.23) | copy-start | bytes 1540

commit v6 on v5

--- a/solution.py
+++ b/solution.py
@@ -376,14 +376,11 @@
         )
 
     def start_halo(tab, layer):
-        def one(r, carry):
+        for r in range(1, ngraph):
             p = gpeer(r)
             halo[layer, p] = select_rows(tab, high_ref[p], low_ref[p])
             for copy in halo_copies(tab, layer, r):
                 copy.start()
-            return carry
-
-        lax.fori_loop(1, ngraph, one, 0)
         tab[pl.ds(pl.multiple_of(hub_base + g * per, per), per)] = select_rows(tab, high_ref[g, nsend:], low_ref[g, nsend:])
 
     def wait_halo(tab, layer):
@@ -490,12 +487,12 @@
                 hin[f, chunk(i)] = h
 
     far1(0)
+    own_blocks(tab1, 0, [q * nchunk + nchunk - 1 for q in range(nfeat)])
     hub_totals(0)
     for copy in w2_copies:
         copy.wait_recv()
 
     finish1(0)
-    own_blocks(tab1, 0, [q * nchunk + nchunk - 1 for q in range(nfeat)])
     far1(1)
 
     def rows1(i, carry):
@@ -596,7 +593,7 @@
             dma(nblk), dma(fr), dma(fr), dma(nchunk, fr), dma(nchunk, fr),
             dma(2, gr), dma(2, gr), dma(2, gr), dma(2, gr), dma(2, gr), dma(2, gr), dma(nchunk, fr), dma(nchunk, fr),
         ],
-        compiler_params=pltpu.CompilerParams(collective_id=1, has_side_effects=True, vmem_limit_bytes=52 * 2**20),
+        compiler_params=pltpu.CompilerParams(collective_id=1, has_side_effects=True, vmem_limit_bytes=48 * 2**20),
         name="layers",
     )(tab_own, w2, high, low, myhub, b1, inv, adj)
 

time: 114 us -> 112 us (0.982)
  other arithmetic: 2.26 us -> 1.04 us
    add x1, other arithmetic: 2.26 us -> 1.04 us  [device_program(): run_layers(nfeat, ngraph, nsend, per, tab_own, w_second, high, low, myhub...]
where the time goes in v6:
time: 112 us
  Pallas kernels  111 us (99%)
    pallas_call x1, Pallas kernels, run_layers(): pl.pallas_call(functools.partial(layers_kernel, (nfeat, ngraph, vert, nse...  60.2 us
    pallas_call x1, Pallas kernels, build_adjacency(): pl.pallas_call(functools.partial(build_kernel, ndb, nsb, ncol), out_shape...  26 us
    pallas_call x1, Pallas kernels, run_pre(): pl.pallas_call(functools.partial(pre_kernel, (nfeat, ngraph, ndb, nsb)),...  25.1 us

profile of v6, /device:TPU:97, one launch (start us, length us, event | category | flops | bytes accessed | tf_op | source)
XLA Modules:
  0.0 112.4 jit_solution(10790386802197751117)
XLA Ops:
  0.0 0.0 copy-start.4
  0.0 0.0 copy-start.3
  0.0 25.1 %pre.1 = (f32[2624,128]{1,0:T(8,128)}, s32[8,384]{1,0:T(8,128)}, bf16[2048,128]{1,0:T(8,128)(2,1)}, f32[1,128]{1,0:T(1,128)}, f32[128,128]{1,0:T(8,128)}, /*inde...) custom-call(s32[320,128]{1,0:T(8,128)} %bitcast.9, s32[320,128]{1,0:T(8,128)} %bitcast.10, ...), custom_call_target="tpu_custom_call" | custom-call | tf_op jit(solution)/shard_map/pre/pallas_call | solution.py:304
  25.1 0.0 copy-start
  25.1 0.0 copy-start.1
  25.1 0.0 copy-start.2
  25.1 0.0 copy-start.5
  25.1 0.0 copy-start.6
  25.1 0.0 copy-start.7
  25.1 26.0 %build.1.a_hbm = f32[2176,4224]{1,0:T(8,128)} custom-call(s32[8,384]{1,0:T(8,128)} %get-tuple-element.18.starts_ref, f32[2624,128]{1,0:T(8,128)} %get-tuple-element.19.edges_ref, f32[128,128]{1,0:T(8,128)} %get-tuple-element.20.hubcol_ref), custom_call_target="tpu_custom_call" | custom-call | tf_op jit(solution)/shard_map/build/pallas_call | solution.py:72
  51.2 0.0 copy-done.4
  51.2 0.0 copy-done.3
  51.2 0.0 copy-done
  51.2 0.0 copy-done.1
  51.2 0.0 copy-done.2
  51.2 0.0 copy-done.5
  51.2 0.0 copy-done.6
  51.2 60.2 %layers.1 = f32[2048,128]{1,0:T(8,128)S(1)} custom-call(bf16[2048,128]{1,0:T(8,128)(2,1)S(1)} %copy-done.2, bf16[128,512]{1,0:T(8,128)(2,1)S(1)} %copy-done.3, bf16[8,272,128]{2,1,0:T(8,128)(2,1)S(1)} %copy-done, bf16[8,272,128]{2,1,0:T(8,128)(2,1)S(1)} %copy-done.1, s32[1,128]{1,0:T(1,128)S(1)} %copy-done.6, f32[1,128]{1,0:T(1,128)S(1)} %bitcast.7, ...), custom_call_target="tpu_custom_call" | custom-call | tf_op jit(solution)/shard_map/layers/pallas_call | solution.py:584
  111.4 0.0 copy-done.7
  111.4 1.0 broadcast_add_fusion
Async XLA Ops:
  0.0 51.2 %copy-start.4 = (f32[128]{0:T(128)S(1)}, f32[128]{0:T(128)}, u32[]{:S(2)}) copy-start(f32[128]{0:T(128)} %param.22) | copy-start | bytes 1540
  0.0 51.2 %copy-start.3 = (bf16[128,512]{1,0:T(8,128)(2,1)S(1)}, bf16[128,512]{1,0:T(8,128)(2,1)}, u32[]{:S(2)}) copy-start(bf16[128,512]{1,0:T(8,128)(2,1)} %w2_ref.1) | copy-start | bytes 393220
  25.1 26.1 %copy-start = (bf16[8,272,128]{2,1,0:T(8,128)(2,1)S(1)}, bf16[8,272,128]{2,1,0:T(8,128)(2,1)}, u32[]{:S(2)}) copy-start(bf16[8,272,128]{2,1,0:T(8,128)(2,1)} %get-tuple-element.14.high_ref) | copy-start | bytes 1671172
  25.1 26.1 %copy-start.1 = (bf16[8,272,128]{2,1,0:T(8,128)(2,1)S(1)}, bf16[8,272,128]{2,1,0:T(8,128)(2,1)}, u32[]{:S(2)}) copy-start(bf16[8,272,128]{2,1,0:T(8,128)(2,1)} %get-tuple-element.15.low_ref) | copy-start | bytes 1671172
  25.1 26.1 %copy-start.2 = (bf16[2048,128]{1,0:T(8,128)(2,1)S(1)}, bf16[2048,128]{1,0:T(8,128)(2,1)}, u32[]{:S(2)}) copy-start(bf16[2048,128]{1,0:T(8,128)(2,1)} %get-tuple-element.13.tabown_ref) | copy-start | bytes 1572868
  25.1 26.1 %copy-start.5 = (f32[1,128]{1,0:T(1,128)S(1)}, f32[1,128]{1,0:T(1,128)}, u32[]{:S(2)}) copy-start(f32[1,128]{1,0:T(1,128)} %get-tuple-element.17.inv_ref) | copy-start | bytes 1540
  25.1 26.1 %copy-start.6 = (s32[1,128]{1,0:T(1,128)S(1)}, s32[1,128]{1,0:T(1,128)}, u32[]{:S(2)}) copy-start(s32[1,128]{1,0:T(1,128)} %get-tuple-element.16.myhub_ref) | copy-start | bytes 1540
  25.1 86.3 %copy-start.7 = (f32[128]{0:T(128)S(1)}, f32[128]{0:T(128)}, u32[]{:S(2)}) copy-start(f32[128]{0:T(128)} %param.23) | copy-start | bytes 1540
